TPU v7x, 512 devices: a whole 4x4x16 slice. The times are simulated.
512 devices in a mesh: gx: 16 (over z_lo, core), gy: 32 (over x, z_hi, y).
Axes of the slice: x: 4, y: 4, z: 16 (z_hi: 2, z_lo: 8; z = z_hi * 8 + z_lo), core: 2. Of those that a mesh axis runs over, the one named last changes fastest.
Arguments:
- green_ops: bfloat16 [16, 32, 2, 1024, 1024], P('gx', 'gy'), may hold values from -0.125 to 0.125
- cell_map: int32 [16, 32, 1024], P('gx', 'gy'), may hold values from 0 to 2
- dipole_site: int32 [16, 32, 128], P('gx', 'gy'), may hold values from 0 to 1023
- dipole_amp: float32 [16, 32, 2, 128], P('gx', 'gy'), may hold values from -32 to 32
- contrast: float32 [3, 2], replicated, may hold values from 0.3 to 1
Outputs:
- traces: bfloat16 [16, 32, 1024, 2, 128], P('gx', 'gy')
All inputs are finite; a program needn't handle non-finite values.
Results may differ from a plain program's by a relative error of at most 0.0069.
Values may be sent and summed in bfloat16 or wider, within the bound.
No kernel may reach another device: no remote copies, remote signals or barrier semaphores. Data moves between devices by JAX's collectives and lax.ppermute only.
A program may use at most 64 MiB of HBM per device.

v0:
```python
import jax
import jax.numpy as jnp
from jax import lax
from jax.sharding import PartitionSpec as P

NB = 64
MB = 2
STEPS = 4


def from_behind(block, axis, distance):
    devices = range(lax.axis_size(axis))
    route = [(i - distance, i) for i in devices if i - distance in devices]
    return lax.ppermute(block, axis, route)


def combine(product):
    real_out = product[0, :, 0] - product[1, :, 1]
    imag_out = product[0, :, 1] + product[1, :, 0]
    return jnp.stack([real_out, imag_out], axis=1).astype(jnp.bfloat16)


def per_device(green_ops, cell_map, dipole_site, dipole_amp, contrast):
    operator = green_ops[0, 0]
    cells = cell_map[0, 0]
    sites = dipole_site[0, 0]
    amplitude = dipole_amp[0, 0]
    trace_rows = operator.shape[1]
    face_rows = trace_rows // 2
    columns = sites.shape[0]
    one_hot = (lax.broadcasted_iota(jnp.int32, (trace_rows, columns), 0) == sites[None, :]).astype(
        jnp.float32
    )
    source = one_hot[:, None, :] * amplitude[None, :, :]
    lookup_table = (
        lax.broadcasted_iota(jnp.int32, (trace_rows, contrast.shape[0]), 1) == cells[:, None]
    ).astype(jnp.float32)
    factor = jnp.dot(lookup_table, contrast, precision=lax.Precision.HIGHEST)
    real_factor = factor[:, 0:1]
    imag_factor = factor[:, 1:2]
    east_trace = jnp.zeros((face_rows, 2, 0), jnp.bfloat16)
    north_trace = jnp.zeros((face_rows, 2, 0), jnp.bfloat16)
    for turn_index in range(STEPS):
        width_live = min(turn_index + 1, MB) * NB
        width_held = east_trace.shape[2]
        if width_held > 0:
            west_trace = from_behind(east_trace, "gx", 1)
            south_trace = from_behind(north_trace, "gy", 1)
        else:
            west_trace = east_trace
            south_trace = north_trace
        padding = ((0, 0), (0, 0), (0, width_live - width_held))
        west_trace = jnp.pad(west_trace, padding)
        south_trace = jnp.pad(south_trace, padding)
        incoming = jnp.concatenate([west_trace, south_trace], axis=0).astype(jnp.float32)
        real_in = (
            real_factor * incoming[:, 0] - imag_factor * incoming[:, 1] + source[:, 0, :width_live]
        )
        imag_in = (
            real_factor * incoming[:, 1] + imag_factor * incoming[:, 0] + source[:, 1, :width_live]
        )
        excited = jnp.stack([real_in, imag_in], axis=1).astype(jnp.bfloat16)
        image_width_live = excited.shape[2]
        flat = excited.reshape(trace_rows, 2 * image_width_live)
        product = jnp.einsum("spq,qc->spc", operator, flat, preferred_element_type=jnp.float32)
        image = combine(product.reshape(2, trace_rows - 0, 2, image_width_live))
        east_trace = image[:face_rows]
        north_trace = image[face_rows:]
    padding = ((0, 0), (0, 0), (0, columns - east_trace.shape[2]))
    traces = jnp.concatenate([east_trace, north_trace], axis=0)
    return traces[None, None]


def solution(mesh):
    placed = (
        P("gx", "gy", None, None, None),
        P("gx", "gy", None),
        P("gx", "gy", None),
        P("gx", "gy", None, None),
        P(),
    )
    return jax.shard_map(
        per_device,
        mesh=mesh,
        in_specs=placed,
        out_specs=P("gx", "gy", None, None, None),
        check_vma=False,
    )
```

profile of v0, /device:TPU:7, one launch (start us, length us, event | category | flops | bytes accessed | tf_op | source)
XLA Modules:
  0.0 116.9 jit_solution(13016438277929224936)
XLA Ops:
  0.0 0.0 copy-start
  0.0 0.7 copy-done
  0.7 1.1 fusion.17
  1.8 0.8 fusion.16
  2.6 0.8 broadcast_multiply_fusion
  3.5 3.7 %fusion.6 = f32[128,2,1024]{2,0,1:T(8,128)S(1)} fusion(bf16[1024,128,1]{0,1,2:T(8,128)(2,1)S(1)} %bitcast.63, bf16[1,1,2,1024,1024]{4,3,2,1,0:T(8,128)(2,1)} %param.5), kind=kOutput, calls=%fused_computation.6 | convolution fusion | flops 536870912 | bytes 5505024 | tf_op jit(solution)/shard_map/spq,qc->spc/dot_general | solution.py:65
  7.3 0.0 copy-start.1
  7.3 0.1 fusion.32
  7.4 4.4 %collective-permute-start = (bf16[512,2,64]{0,2,1:T(8,128)(2,1)S(1)}, bf16[512,2,64]{0,2,1:T(8,128)(2,1)S(1)}, u32[]{:S(2)}, u32[]{:S(2)}) collective-permute-start(bf16[512,2,64]{0,2,1:T(8,128)(2,1)S(1)} %get-tuple-element.27), channel_id=1, source_target_pairs={{0,32},{32,64},{64,96},{96,128},{128,160},{160,192},{192,224},{224... | collective-permute-start | bytes 393224 | tf_op jit(solution)/shard_map/ppermute | solution.py:14
  11.7 3.2 %collective-permute-start.1 = (bf16[512,2,64]{0,2,1:T(8,128)(2,1)S(1)}, bf16[512,2,64]{0,2,1:T(8,128)(2,1)S(1)}, u32[]{:S(2)}, u32[]{:S(2)}) collective-permute-start(bf16[512,2,64]{0,2,1:T(8,128)(2,1)S(1)} %get-tuple-element.28), channel_id=1, source_target_pairs={{0,1},{1,2},{2,3},{3,4},{4,5},{5,6},{6,7},{7,8},{8,9},{9,10},{10,1... | collective-permute-start | bytes 393224 | tf_op jit(solution)/shard_map/ppermute | solution.py:14
  14.9 0.0 collective-permute-done
  15.0 17.6 %collective-permute-done.1 = bf16[512,2,64]{0,2,1:T(8,128)(2,1)S(1)} collective-permute-done((bf16[512,2,64]{0,2,1:T(8,128)(2,1)S(1)}, bf16[512,2,64]{0,2,1:T(8,128)(2,1)S(1)}, u32[]{:S(2)}, u32[]{:S(2)}) %collective-permute-start.1) | collective-permute-done | bytes 131104 | tf_op jit(solution)/shard_map/ppermute | solution.py:14
  32.5 0.1 fusion.11
  32.6 0.2 add_convert_fusion.6
  32.9 0.1 pad_maximum_fusion
  32.9 0.0 copy-done.1
  32.9 1.3 %fusion.4 = f32[256,2,1024]{2,0,1:T(8,128)S(1)} fusion(bf16[1024,256,1]{0,1,2:T(8,128)(2,1)S(1)} %bitcast.64, bf16[1,1,2,1024,1024]{4,3,2,1,0:T(8,128)(2,1)S(1)} %copy-done.1), kind=kOutput, calls=%fused_computation.4 | convolution fusion | flops 1073741824 | bytes 6815744 | tf_op jit(solution)/shard_map/spq,qc->spc/dot_general | solution.py:65
  34.2 0.1 fusion.22
  34.4 10.8 %collective-permute-start.2 = (bf16[512,2,128]{0,2,1:T(8,128)(2,1)S(1)}, bf16[512,2,128]{0,2,1:T(8,128)(2,1)S(1)}, u32[]{:S(2)}, u32[]{:S(2)}) collective-permute-start(bf16[512,2,128]{0,2,1:T(8,128)(2,1)S(1)} %get-tuple-element.25), channel_id=1, source_target_pairs={{0,32},{32,64},{64,96},{96,128},{128,160},{160,192},{192,224},{224... | collective-permute-start | bytes 786440 | tf_op jit(solution)/shard_map/ppermute | solution.py:14
  45.3 1.9 %collective-permute-start.3 = (bf16[512,2,128]{0,2,1:T(8,128)(2,1)S(1)}, bf16[512,2,128]{0,2,1:T(8,128)(2,1)S(1)}, u32[]{:S(2)}, u32[]{:S(2)}) collective-permute-start(bf16[512,2,128]{0,2,1:T(8,128)(2,1)S(1)} %get-tuple-element.26), channel_id=1, source_target_pairs={{0,1},{1,2},{2,3},{3,4},{4,5},{5,6},{6,7},{7,8},{8,9},{9,10},{10,1... | collective-permute-start | bytes 786440 | tf_op jit(solution)/shard_map/ppermute | solution.py:14
  47.2 1.4 %collective-permute-done.2 = bf16[512,2,128]{0,2,1:T(8,128)(2,1)S(1)} collective-permute-done((bf16[512,2,128]{0,2,1:T(8,128)(2,1)S(1)}, bf16[512,2,128]{0,2,1:T(8,128)(2,1)S(1)}, u32[]{:S(2)}, u32[]{:S(2)}) %collective-permute-start.2) | collective-permute-done | bytes 262176 | tf_op jit(solution)/shard_map/ppermute | solution.py:14
  48.6 15.9 %collective-permute-done.3 = bf16[512,2,128]{0,2,1:T(8,128)(2,1)S(1)} collective-permute-done((bf16[512,2,128]{0,2,1:T(8,128)(2,1)S(1)}, bf16[512,2,128]{0,2,1:T(8,128)(2,1)S(1)}, u32[]{:S(2)}, u32[]{:S(2)}) %collective-permute-start.3) | collective-permute-done | bytes 262176 | tf_op jit(solution)/shard_map/ppermute | solution.py:14
  64.4 0.1 maximum_convert_fusion
  64.5 0.2 add_convert_fusion.4
  64.8 0.1 pad_maximum_fusion.1
  64.9 1.3 %fusion.2 = f32[256,2,1024]{2,0,1:T(8,128)S(1)} fusion(bf16[1024,256,1]{0,1,2:T(8,128)(2,1)S(1)} %bitcast.65, bf16[1,1,2,1024,1024]{4,3,2,1,0:T(8,128)(2,1)S(1)} %copy-done.1), kind=kOutput, calls=%fused_computation.2 | convolution fusion | flops 1073741824 | bytes 6815744 | tf_op jit(solution)/shard_map/spq,qc->spc/dot_general | solution.py:65
  66.2 0.1 fusion.24
  66.3 16.6 %collective-permute-start.4 = (bf16[512,2,128]{0,2,1:T(8,128)(2,1)S(1)}, bf16[512,2,128]{0,2,1:T(8,128)(2,1)S(1)}, u32[]{:S(2)}, u32[]{:S(2)}) collective-permute-start(bf16[512,2,128]{0,2,1:T(8,128)(2,1)S(1)} %get-tuple-element.23), channel_id=1, source_target_pairs={{0,32},{32,64},{64,96},{96,128},{128,160},{160,192},{192,224},{224... | collective-permute-start | bytes 786440 | tf_op jit(solution)/shard_map/ppermute | solution.py:14
  83.0 1.9 %collective-permute-start.5 = (bf16[512,2,128]{0,2,1:T(8,128)(2,1)S(1)}, bf16[512,2,128]{0,2,1:T(8,128)(2,1)S(1)}, u32[]{:S(2)}, u32[]{:S(2)}) collective-permute-start(bf16[512,2,128]{0,2,1:T(8,128)(2,1)S(1)} %get-tuple-element.24), channel_id=1, source_target_pairs={{0,1},{1,2},{2,3},{3,4},{4,5},{5,6},{6,7},{7,8},{8,9},{9,10},{10,1... | collective-permute-start | bytes 786440 | tf_op jit(solution)/shard_map/ppermute | solution.py:14
  84.9 1.4 %collective-permute-done.4 = bf16[512,2,128]{0,2,1:T(8,128)(2,1)S(1)} collective-permute-done((bf16[512,2,128]{0,2,1:T(8,128)(2,1)S(1)}, bf16[512,2,128]{0,2,1:T(8,128)(2,1)S(1)}, u32[]{:S(2)}, u32[]{:S(2)}) %collective-permute-start.4) | collective-permute-done | bytes 262176 | tf_op jit(solution)/shard_map/ppermute | solution.py:14
  86.3 26.5 %collective-permute-done.5 = bf16[512,2,128]{0,2,1:T(8,128)(2,1)S(1)} collective-permute-done((bf16[512,2,128]{0,2,1:T(8,128)(2,1)S(1)}, bf16[512,2,128]{0,2,1:T(8,128)(2,1)S(1)}, u32[]{:S(2)}, u32[]{:S(2)}) %collective-permute-start.5) | collective-permute-done | bytes 262176 | tf_op jit(solution)/shard_map/ppermute | solution.py:14
  112.7 0.1 maximum_convert_fusion.1
  112.9 0.2 add_convert_fusion.2
  113.1 0.1 pad_maximum_fusion.2
  113.2 1.3 %fusion = f32[256,2,1024]{2,0,1:T(8,128)S(1)} fusion(bf16[1024,256,1]{0,1,2:T(8,128)(2,1)S(1)} %bitcast.66, bf16[1,1,2,1024,1024]{4,3,2,1,0:T(8,128)(2,1)S(1)} %copy-done.1), kind=kOutput, calls=%fused_computation | convolution fusion | flops 1073741824 | bytes 6815744 | tf_op jit(solution)/shard_map/spq,qc->spc/dot_general | solution.py:65
  114.5 0.1 fusion.36
  114.6 0.2 copy.16
  114.8 0.2 copy.17
  115.0 0.2 copy.15
  115.2 0.2 copy.18
  115.4 0.1 fusion.18
  115.5 0.1 pad_maximum_fusion.3
  115.6 1.3 %copy.14 = bf16[1,1,1024,2,128]{4,3,2,1,0:T(2,128)(2,1)} copy(bf16[1,1,1024,2,128]{4,2,3,1,0:T(8,128)(2,1)S(1)} %pad_maximum_fusion.3) | data formatting | bytes 1048576 | tf_op jit(solution)/shard_map/stack | solution.py:20
  (8 shorter events, 0.2 us)
Async XLA Ops:
  0.0 0.7 copy-start
  7.3 25.7 %copy-start.1 = (bf16[1,1,2,1024,1024]{4,3,2,1,0:T(8,128)(2,1)S(1)}, bf16[1,1,2,1024,1024]{4,3,2,1,0:T(8,128)(2,1)}, u32[]{:S(2)}) copy-start(bf16[1,1,2,1024,1024]{4,3,2,1,0:T(8,128)(2,1)} %param.5) | copy-start | bytes 12582916
  7.4 7.6 %collective-permute-start = (bf16[512,2,64]{0,2,1:T(8,128)(2,1)S(1)}, bf16[512,2,64]{0,2,1:T(8,128)(2,1)S(1)}, u32[]{:S(2)}, u32[]{:S(2)}) collective-permute-start(bf16[512,2,64]{0,2,1:T(8,128)(2,1)S(1)} %get-tuple-element.27), channel_id=1, source_target_pairs={{0,32},{32,64},{64,96},{96,128},{128,160},{160,192},{192,224},{224... | collective-permute-start | bytes 393224 | tf_op jit(solution)/shard_map/ppermute | solution.py:14
  11.7 20.8 %collective-permute-start.1 = (bf16[512,2,64]{0,2,1:T(8,128)(2,1)S(1)}, bf16[512,2,64]{0,2,1:T(8,128)(2,1)S(1)}, u32[]{:S(2)}, u32[]{:S(2)}) collective-permute-start(bf16[512,2,64]{0,2,1:T(8,128)(2,1)S(1)} %get-tuple-element.28), channel_id=1, source_target_pairs={{0,1},{1,2},{2,3},{3,4},{4,5},{5,6},{6,7},{7,8},{8,9},{9,10},{10,1... | collective-permute-start | bytes 393224 | tf_op jit(solution)/shard_map/ppermute | solution.py:14
  34.4 14.1 %collective-permute-start.2 = (bf16[512,2,128]{0,2,1:T(8,128)(2,1)S(1)}, bf16[512,2,128]{0,2,1:T(8,128)(2,1)S(1)}, u32[]{:S(2)}, u32[]{:S(2)}) collective-permute-start(bf16[512,2,128]{0,2,1:T(8,128)(2,1)S(1)} %get-tuple-element.25), channel_id=1, source_target_pairs={{0,32},{32,64},{64,96},{96,128},{128,160},{160,192},{192,224},{224... | collective-permute-start | bytes 786440 | tf_op jit(solution)/shard_map/ppermute | solution.py:14
  45.3 19.2 %collective-permute-start.3 = (bf16[512,2,128]{0,2,1:T(8,128)(2,1)S(1)}, bf16[512,2,128]{0,2,1:T(8,128)(2,1)S(1)}, u32[]{:S(2)}, u32[]{:S(2)}) collective-permute-start(bf16[512,2,128]{0,2,1:T(8,128)(2,1)S(1)} %get-tuple-element.26), channel_id=1, source_target_pairs={{0,1},{1,2},{2,3},{3,4},{4,5},{5,6},{6,7},{7,8},{8,9},{9,10},{10,1... | collective-permute-start | bytes 786440 | tf_op jit(solution)/shard_map/ppermute | solution.py:14
  66.3 19.9 %collective-permute-start.4 = (bf16[512,2,128]{0,2,1:T(8,128)(2,1)S(1)}, bf16[512,2,128]{0,2,1:T(8,128)(2,1)S(1)}, u32[]{:S(2)}, u32[]{:S(2)}) collective-permute-start(bf16[512,2,128]{0,2,1:T(8,128)(2,1)S(1)} %get-tuple-element.23), channel_id=1, source_target_pairs={{0,32},{32,64},{64,96},{96,128},{128,160},{160,192},{192,224},{224... | collective-permute-start | bytes 786440 | tf_op jit(solution)/shard_map/ppermute | solution.py:14
  83.0 29.8 %collective-permute-start.5 = (bf16[512,2,128]{0,2,1:T(8,128)(2,1)S(1)}, bf16[512,2,128]{0,2,1:T(8,128)(2,1)S(1)}, u32[]{:S(2)}, u32[]{:S(2)}) collective-permute-start(bf16[512,2,128]{0,2,1:T(8,128)(2,1)S(1)} %get-tuple-element.24), channel_id=1, source_target_pairs={{0,1},{1,2},{2,3},{3,4},{4,5},{5,6},{6,7},{7,8},{8,9},{9,10},{10,1... | collective-permute-start | bytes 786440 | tf_op jit(solution)/shard_map/ppermute | solution.py:14
where the time goes:
time: 117 us
  waiting for transfers between devices  62.7 us (54%)
  starting transfers between devices  38.8 us (33%)
  matrix products  8.72 us (7%)
  other arithmetic  3.43 us (3%)
  local copies, waits for them, and re-layouts  2.95 us (3%)
    ppermute x6, waiting for transfers between devices, from_behind(): return lax.ppermute(block, axis, route)  62.7 us
    ppermute x6, starting transfers between devices, from_behind(): return lax.ppermute(block, axis, route)  38.8 us
    dot_general x4, matrix products, per_device(): jnp.einsum('spq,qc->spc', operator, flat, preferred_element_type=jnp.floa...  7.6 us
  transfers between devices with their start and end apart: 6, of which 5 were waited for; matrix products, arithmetic and copies ran while one was open for 0% of the time, Pallas kernels for 0%

commit v1 on v0

v1 whole, which is shorter than its diff:
```python
import jax
import jax.numpy as jnp
from jax import lax
from jax.sharding import PartitionSpec as P


NB = 64
BLOCK = 4
PIECES = ((3, 48), (1, 40), (0, 40))


def per_device(green_ops, cell_map, dipole_site, dipole_amp, contrast):
    operator = green_ops[0, 0]
    cells = cell_map[0]
    sites = dipole_site[0, 0]
    amplitude = dipole_amp[0, 0]
    rows = operator.shape[1]
    face = rows // 2
    width = sites.shape[0]
    n_gx = lax.axis_size("gx")
    n_gy = lax.axis_size("gy")
    blocks = n_gy // BLOCK
    lane = lax.axis_index("gy") % BLOCK

    hot = lax.broadcasted_iota(jnp.int32, (width, rows), 1) == sites[:, None]
    source = jnp.where(hot[None], amplitude[:, :, None], 0.0)

    def factor_of(part):
        return jnp.where(
            cells == 0, contrast[0, part], jnp.where(cells == 1, contrast[1, part], contrast[2, part])
        )

    real_factor = factor_of(0)
    imag_factor = factor_of(1)

    def apply(excited):
        live = excited.shape[1]
        flat = excited.reshape(2 * live, rows)
        product = lax.dot_general(
            flat, operator, (((1,), (2,)), ((), ())), preferred_element_type=jnp.float32
        )
        product = product.reshape(2, live, 2, rows)
        real_out = product[0, :, 0] - product[1, :, 1]
        imag_out = product[1, :, 0] + product[0, :, 1]
        return jnp.stack([real_out, imag_out]).astype(jnp.bfloat16)

    def step(west, south):
        incoming = jnp.concatenate([west, south], axis=2).astype(jnp.float32)
        live = incoming.shape[1]
        real_in = real_factor * incoming[0] - imag_factor * incoming[1] + source[0, :live]
        imag_in = real_factor * incoming[1] + imag_factor * incoming[0] + source[1, :live]
        return apply(jnp.stack([real_in, imag_in]).astype(jnp.bfloat16))

    def east_to(traces, lanes):
        pairs = [
            (i * n_gy + j, (i + 1) * n_gy + j)
            for i in range(n_gx - 1)
            for j in range(n_gy)
            if j % BLOCK in lanes
        ]
        return lax.ppermute(traces[:, :, :face], ("gx", "gy"), pairs)

    def north_to(traces, lanes):
        pairs = [(j, j + 1) for j in range(n_gy) if j % BLOCK in lanes]
        return lax.ppermute(traces[:, :, face:], "gy", pairs)

    def cross(traces):
        north = traces[:, :, face:]
        live = north.shape[1]
        at = 0
        pieces = []
        for column, share in PIECES:
            size = share * live // width
            pieces.append((column, north[:, at : at + size]))
            at += size
        moved = []
        for column, piece in pieces:
            if column != BLOCK - 1:
                pairs = [(b * BLOCK + BLOCK - 1, b * BLOCK + column) for b in range(blocks - 1)]
                piece = lax.ppermute(piece, "gy", pairs)
            moved.append((column, piece))
        arrived = []
        for column, piece in moved:
            pairs = [(b * BLOCK + column, (b + 1) * BLOCK) for b in range(blocks - 1)]
            arrived.append(lax.ppermute(piece, "gy", pairs))
        return jnp.concatenate(arrived, axis=1)

    t0 = apply(source.astype(jnp.bfloat16))
    w1 = east_to(t0, (0, 1, 2, 3))
    s1 = north_to(t0, (0, 1, 2))
    x1 = cross(t0)

    t1 = step(w1, s1)
    w2 = east_to(t1, (1, 2, 3))
    s2 = north_to(t1, (1, 2))
    x2 = cross(t1)

    t2 = step(jnp.where(lane == 0, w1, w2), jnp.where(lane == 0, x1, s2))
    w3 = east_to(t2, (0, 2, 3))
    s3 = north_to(t2, (0, 2))
    x3 = cross(t2[:, :NB])

    t3 = step(jnp.where(lane == 1, w2, w3), jnp.where(lane == 0, x2, s3))
    w4 = east_to(t3[:, :NB], (0, 1))
    s4 = north_to(t3[:, :NB], (0, 1))

    t4 = step(jnp.where(lane == 2, w3[:, :NB], w4), jnp.where(lane == 0, x3, s4))

    first = jnp.where(lane == 3, t3[:, :NB], t4)
    second = jnp.where(lane >= 2, t2[:, NB:], t3[:, NB:])
    traces = jnp.concatenate([first, second], axis=1)
    return traces.transpose(2, 0, 1)[None, None]


def solution(mesh):
    placed = (
        P("gx", "gy", None, None, None),
        P("gx", "gy", None),
        P("gx", "gy", None),
        P("gx", "gy", None, None),
        P(),
    )
    return jax.shard_map(
        per_device,
        mesh=mesh,
        in_specs=placed,
        out_specs=P("gx", "gy", None, None, None),
        check_vma=False,
    )
```

time: 117 us -> 118 us (level)
  waiting for transfers between devices: 62.7 us -> 48.4 us
  starting transfers between devices: 38.8 us -> 49.9 us
  other arithmetic: 3.43 us -> 7.17 us
    ppermute x6 -> x23, waiting for transfers between devices: 62.7 us -> 48.4 us  [the longest x9 37.6 us: cross(): arrived.append(lax.ppermute(piece, 'gy', pairs))]
    ppermute x6 -> x23, starting transfers between devices: 38.8 us -> 49.9 us  [the longest x9 22.6 us: cross(): arrived.append(lax.ppermute(piece, 'gy', pairs))]
    select_n x0 -> x9, other arithmetic: none -> 4.33 us  [the longest x1 3.72 us: factor_of(): jnp.where(cells == 0, contrast[0, part], jnp.where(cells == 1, contrast[1...]
    unnamed x8 -> x12, local copies, waits for them, and re-layouts: 1.46 us -> 0.04 us
    another operation x1 -> x0, local copies, waits for them, and re-layouts: 1.33 us -> none  [combine(): return jnp.stack([real_out, imag_out], axis=1).astype(jnp.bfloat16)]
  transfers between devices with their start and end apart: 6 -> 23, of which waited for: 5 -> 10; matrix products, arithmetic and copies ran while one was open for 0% -> 4% of each run, Pallas kernels for 0% -> 0%
where the time goes in v1:
time: 118 us; the launch traced here: 117 us
  starting transfers between devices  49.9 us (42%)
  waiting for transfers between devices  48.4 us (41%)
  matrix products  8.89 us (8%)
  other arithmetic  7.17 us (6%)
  local copies, waits for them, and re-layouts  1.8 us (2%)
    ppermute x9, waiting for transfers between devices, cross(): arrived.append(lax.ppermute(piece, 'gy', pairs))  37.6 us
    ppermute x9, starting transfers between devices, cross(): arrived.append(lax.ppermute(piece, 'gy', pairs))  22.6 us
    ppermute x4, starting transfers between devices, east_to(): return lax.ppermute(traces[:, :, :face], ('gx', 'gy'), pairs)  14 us
    ppermute x6, waiting for transfers between devices, cross(): piece = lax.ppermute(piece, 'gy', pairs)  10.5 us
    dot_general x5, matrix products, apply(): lax.dot_general(flat, operator, (((1,), (2,)), ((), ())), preferred_eleme...  8.89 us
    ppermute x6, starting transfers between devices, cross(): piece = lax.ppermute(piece, 'gy', pairs)  6.75 us
    ppermute x4, starting transfers between devices, north_to(): return lax.ppermute(traces[:, :, face:], 'gy', pairs)  6.5 us
    select_n x1, other arithmetic, factor_of(): jnp.where(cells == 0, contrast[0, part], jnp.where(cells == 1, contrast[1...  3.72 us
  transfers between devices with their start and end apart: 23, of which 10 were waited for; matrix products, arithmetic and copies ran while one was open for 4% of the time, Pallas kernels for 0%

profile of v1, /device:TPU:7, one launch (start us, length us, event | category | flops | bytes accessed | tf_op | source)
XLA Modules:
  0.0 116.9 jit_solution(13016442786339921262)
XLA Ops:
  0.0 0.8 iota_compare_fusion
  0.8 0.0 copy-start.3
  0.8 0.0 copy-start.4
  0.8 0.0 copy-start.5
  0.8 3.5 %fusion.8 = f32[2,128,2,1024]{3,1,2,0:T(8,128)S(1)} fusion(bf16[1,1,2,1024,1024]{4,3,2,1,0:T(8,128)(2,1)} %param.5, f32[2,128]{1,0:T(2,128)} %bitcast.80, pred[128,1024]{1,0:T(8,128)(4,1)S(1)} %iota_compare_fusion), kind=kOutput, calls=%fused_computation.8 | convolution fusion | flops 1074003968 | bytes 6423552 | tf_op jit(solution)/shard_map/dot_general | solution.py:39
  4.3 0.0 copy-start
  4.4 0.1 fusion.27
  4.6 4.4 %collective-permute-start = (bf16[2,128,512]{2,1,0:T(8,128)(2,1)S(1)}, bf16[2,128,512]{2,1,0:T(8,128)(2,1)S(1)}, u32[]{:S(2)}, u32[]{:S(2)}) collective-permute-start(bf16[2,128,512]{2,1,0:T(8,128)(2,1)S(1)} %get-tuple-element.37), channel_id=1, source_target_pairs={{0,32},{1,33},{2,34},{3,35},{4,36},{5,37},{6,38},{7,39},{8,40},{9,... | collective-permute-start | bytes 786440 | tf_op jit(solution)/shard_map/ppermute | solution.py:61
  8.9 3.2 %collective-permute-start.1 = (bf16[2,128,512]{2,1,0:T(8,128)(2,1)S(1)}, bf16[2,128,512]{2,1,0:T(8,128)(2,1)S(1)}, u32[]{:S(2)}, u32[]{:S(2)}) collective-permute-start(bf16[2,128,512]{2,1,0:T(8,128)(2,1)S(1)} %get-tuple-element.38), channel_id=1, source_target_pairs={{0,1},{1,2},{2,3},{4,5},{5,6},{6,7},{8,9},{9,10},{10,11},{12,13},{... | collective-permute-start | bytes 786440 | tf_op jit(solution)/shard_map/ppermute | solution.py:65
  12.2 0.7 fusion.65
  12.8 3.7 %compare_select_fusion.3 = (f32[1,1,1024]{2,1,0:T(1,128)S(1)}, f32[1,1,1024]{2,1,0:T(1,128)S(1)}) fusion(s32[1,1,1024]{2,1,0:T(1,128)S(1)} %copy-done.4, f32[]{:T(128)} %bitcast.2, f32[]{:T(128)} %bitcast.1, f32[]{:T(128)} %bitcast, f32[]{:T(128)} %bitcast.14, f32[]{:T(128)} %bitcast.13, f32[]{:T(128)} %bitcast.12), kind=kLoop, calls=%fused_computation.134 | loop fusion | flops 6144 | bytes 12312 | tf_op jit(solution)/shard_map/jit(_where)/select_n | solution.py:29
  16.6 0.2 broadcast_select_fusion
  16.7 0.3 collective-permute-done.1
  17.0 0.1 maximum_convert_fusion
  17.1 0.2 add_convert_fusion.5
  17.4 1.3 %fusion.6 = f32[2,128,2,1024]{3,1,2,0:T(8,128)S(1)} fusion(bf16[1,1,2,1024,1024]{4,3,2,1,0:T(8,128)(2,1)S(1)} %copy-done, bf16[1,128,1024]{2,1,0:T(8,128)(2,1)S(1)} %get-tuple-element.10, bf16[1,128,1024]{2,1,0:T(8,128)(2,1)S(1)} %get-tuple-element.9), kind=kOutput, calls=%fused_computation.6 | convolution fusion | flops 1074790400 | bytes 6815744 | tf_op jit(solution)/shard_map/dot_general | solution.py:39
  18.7 0.1 fusion.29
  18.9 0.7 collective-permute-start.2
  19.6 1.3 %collective-permute-start.4 = (bf16[2,40,512]{2,1,0:T(8,128)(2,1)S(1)}, bf16[2,40,512]{2,1,0:T(8,128)(2,1)}, u32[]{:S(2)}, u32[]{:S(2)}) collective-permute-start(bf16[2,40,512]{2,1,0:T(8,128)(2,1)S(1)} %get-tuple-element.35), channel_id=1, source_target_pairs={{3,1},{7,5},{11,9},{15,13},{19,17},{23,21},{27,25},{35,33},{39,37}... | collective-permute-start | bytes 245768 | tf_op jit(solution)/shard_map/ppermute | solution.py:80
  20.9 1.3 %collective-permute-start.6 = (bf16[2,40,512]{2,1,0:T(8,128)(2,1)S(1)}, bf16[2,40,512]{2,1,0:T(8,128)(2,1)}, u32[]{:S(2)}, u32[]{:S(2)}) collective-permute-start(bf16[2,40,512]{2,1,0:T(8,128)(2,1)S(1)} %get-tuple-element.36), channel_id=1, source_target_pairs={{3,0},{7,4},{11,8},{15,12},{19,16},{23,20},{27,24},{35,32},{39,36}... | collective-permute-start | bytes 245768 | tf_op jit(solution)/shard_map/ppermute | solution.py:80
  22.2 0.7 collective-permute-start.8
  22.9 1.3 %collective-permute-start.3 = (bf16[2,48,512]{2,1,0:T(8,128)(2,1)S(1)}, bf16[2,48,512]{2,1,0:T(8,128)(2,1)S(1)}, u32[]{:S(2)}, u32[]{:S(2)}) collective-permute-start(bf16[2,48,512]{2,1,0:T(8,128)(2,1)S(1)} %fusion.54), channel_id=1, source_target_pairs={{3,4},{7,8},{11,12},{15,16},{19,20},{23,24},{27,28},{35,36},{39,40... | collective-permute-start | bytes 294920 | tf_op jit(solution)/shard_map/ppermute | solution.py:85
  24.2 0.0 copy-start.1
  24.2 1.6 %collective-permute-start.5 = (bf16[2,40,512]{2,1,0:T(8,128)(2,1)}, bf16[2,40,512]{2,1,0:T(8,128)(2,1)S(1)}, u32[]{:S(2)}, u32[]{:S(2)}) collective-permute-start(bf16[2,40,512]{2,1,0:T(8,128)(2,1)} %collective-permute-done.4), channel_id=1, source_target_pairs={{1,4},{5,8},{9,12},{13,16},{17,20},{21,24},{25,28},{33,36},{37,40}... | collective-permute-start | bytes 245768 | tf_op jit(solution)/shard_map/ppermute | solution.py:85
  25.8 6.9 %collective-permute-done.6 = bf16[2,40,512]{2,1,0:T(8,128)(2,1)} collective-permute-done((bf16[2,40,512]{2,1,0:T(8,128)(2,1)S(1)}, bf16[2,40,512]{2,1,0:T(8,128)(2,1)}, u32[]{:S(2)}, u32[]{:S(2)}) %collective-permute-start.6) | collective-permute-done | bytes 81952 | tf_op jit(solution)/shard_map/ppermute | solution.py:80
  32.7 8.5 %collective-permute-start.7 = (bf16[2,40,512]{2,1,0:T(8,128)(2,1)}, bf16[2,40,512]{2,1,0:T(8,128)(2,1)S(1)}, u32[]{:S(2)}, u32[]{:S(2)}) collective-permute-start(bf16[2,40,512]{2,1,0:T(8,128)(2,1)} %collective-permute-done.6), channel_id=1, source_target_pairs={{0,4},{4,8},{8,12},{12,16},{16,20},{20,24},{24,28},{32,36},{36,40}... | collective-permute-start | bytes 245768 | tf_op jit(solution)/shard_map/ppermute | solution.py:85
  41.3 13.7 %collective-permute-done.3 = bf16[2,48,512]{2,1,0:T(8,128)(2,1)S(1)} collective-permute-done((bf16[2,48,512]{2,1,0:T(8,128)(2,1)S(1)}, bf16[2,48,512]{2,1,0:T(8,128)(2,1)S(1)}, u32[]{:S(2)}, u32[]{:S(2)}) %collective-permute-start.3) | collective-permute-done | bytes 98336 | tf_op jit(solution)/shard_map/ppermute | solution.py:85
  55.0 0.1 maximum_select_fusion
  55.1 0.1 maximum_convert_fusion.1
  55.2 0.2 add_convert_fusion.3
  55.4 1.3 %fusion.4 = f32[2,128,2,1024]{3,1,2,0:T(8,128)S(1)} fusion(bf16[1,1,2,1024,1024]{4,3,2,1,0:T(8,128)(2,1)S(1)} %copy-done.1, bf16[1,128,1024]{2,1,0:T(8,128)(2,1)S(1)} %get-tuple-element.8, bf16[1,128,1024]{2,1,0:T(8,128)(2,1)S(1)} %get-tuple-element.7), kind=kOutput, calls=%fused_computation.4 | convolution fusion | flops 1074790400 | bytes 6815744 | tf_op jit(solution)/shard_map/dot_general | solution.py:39
  56.7 0.1 fusion.31
  56.9 3.5 %collective-permute-start.9 = (bf16[2,128,512]{2,1,0:T(8,128)(2,1)S(1)}, bf16[2,128,512]{2,1,0:T(8,128)(2,1)S(1)}, u32[]{:S(2)}, u32[]{:S(2)}) collective-permute-start(bf16[2,128,512]{2,1,0:T(8,128)(2,1)S(1)} %get-tuple-element.29), channel_id=1, source_target_pairs={{0,32},{2,34},{3,35},{4,36},{6,38},{7,39},{8,40},{10,42},{11,43},{... | collective-permute-start | bytes 786440 | tf_op jit(solution)/shard_map/ppermute | solution.py:61
  60.4 0.0 copy-start.2
  60.4 0.8 collective-permute-start.11
  61.3 1.4 %collective-permute-start.13 = (bf16[2,40,512]{2,1,0:T(8,128)(2,1)S(1)}, bf16[2,40,512]{2,1,0:T(8,128)(2,1)S(1)}, u32[]{:S(2)}, u32[]{:S(2)}) collective-permute-start(bf16[2,40,512]{2,1,0:T(8,128)(2,1)S(1)} %get-tuple-element.32), channel_id=1, source_target_pairs={{3,0},{7,4},{11,8},{15,12},{19,16},{23,20},{27,24},{35,32},{39,36}... | collective-permute-start | bytes 245768 | tf_op jit(solution)/shard_map/ppermute | solution.py:80
  62.7 1.3 %collective-permute-start.15 = (bf16[2,128,512]{2,1,0:T(8,128)(2,1)S(1)}, bf16[2,128,512]{2,1,0:T(8,128)(2,1)S(1)}, u32[]{:S(2)}, u32[]{:S(2)}) collective-permute-start(bf16[2,128,512]{2,1,0:T(8,128)(2,1)S(1)} %get-tuple-element.30), channel_id=1, source_target_pairs={{0,1},{2,3},{4,5},{6,7},{8,9},{10,11},{12,13},{14,15},{16,17},{18,... | collective-permute-start | bytes 786440 | tf_op jit(solution)/shard_map/ppermute | solution.py:65
  64.0 1.3 %collective-permute-start.10 = (bf16[2,48,512]{2,1,0:T(8,128)(2,1)S(1)}, bf16[2,48,512]{2,1,0:T(8,128)(2,1)S(1)}, u32[]{:S(2)}, u32[]{:S(2)}) collective-permute-start(bf16[2,48,512]{2,1,0:T(8,128)(2,1)S(1)} %fusion.53), channel_id=1, source_target_pairs={{3,4},{7,8},{11,12},{15,16},{19,20},{23,24},{27,28},{35,36},{39,40... | collective-permute-start | bytes 294920 | tf_op jit(solution)/shard_map/ppermute | solution.py:85
  65.3 1.3 %collective-permute-start.12 = (bf16[2,40,512]{2,1,0:T(8,128)(2,1)S(1)}, bf16[2,40,512]{2,1,0:T(8,128)(2,1)S(1)}, u32[]{:S(2)}, u32[]{:S(2)}) collective-permute-start(bf16[2,40,512]{2,1,0:T(8,128)(2,1)S(1)} %collective-permute-done.11), channel_id=1, source_target_pairs={{1,4},{5,8},{9,12},{13,16},{17,20},{21,24},{25,28},{33,36},{37,40}... | collective-permute-start | bytes 245768 | tf_op jit(solution)/shard_map/ppermute | solution.py:85
  66.6 1.4 %collective-permute-done.13 = bf16[2,40,512]{2,1,0:T(8,128)(2,1)S(1)} collective-permute-done((bf16[2,40,512]{2,1,0:T(8,128)(2,1)S(1)}, bf16[2,40,512]{2,1,0:T(8,128)(2,1)S(1)}, u32[]{:S(2)}, u32[]{:S(2)}) %collective-permute-start.13) | collective-permute-done | bytes 81952 | tf_op jit(solution)/shard_map/ppermute | solution.py:80
  68.1 4.2 %collective-permute-start.14 = (bf16[2,40,512]{2,1,0:T(8,128)(2,1)S(1)}, bf16[2,40,512]{2,1,0:T(8,128)(2,1)S(1)}, u32[]{:S(2)}, u32[]{:S(2)}) collective-permute-start(bf16[2,40,512]{2,1,0:T(8,128)(2,1)S(1)} %collective-permute-done.13), channel_id=1, source_target_pairs={{0,4},{4,8},{8,12},{12,16},{16,20},{20,24},{24,28},{32,36},{36,40}... | collective-permute-start | bytes 245768 | tf_op jit(solution)/shard_map/ppermute | solution.py:85
  72.3 12.5 %collective-permute-done.10 = bf16[2,48,512]{2,1,0:T(8,128)(2,1)S(1)} collective-permute-done((bf16[2,48,512]{2,1,0:T(8,128)(2,1)S(1)}, bf16[2,48,512]{2,1,0:T(8,128)(2,1)S(1)}, u32[]{:S(2)}, u32[]{:S(2)}) %collective-permute-start.10) | collective-permute-done | bytes 98336 | tf_op jit(solution)/shard_map/ppermute | solution.py:85
  84.8 0.2 collective-permute-done.14
  85.0 0.1 maximum_select_fusion.1
  85.1 0.1 maximum_convert_fusion.2
  85.2 0.2 add_convert_fusion.1
  85.4 1.3 %fusion.2 = f32[2,128,2,1024]{3,1,2,0:T(8,128)S(1)} fusion(bf16[1,1,2,1024,1024]{4,3,2,1,0:T(8,128)(2,1)S(1)} %copy-done.2, bf16[1,128,1024]{2,1,0:T(8,128)(2,1)S(1)} %get-tuple-element.6, bf16[1,128,1024]{2,1,0:T(8,128)(2,1)S(1)} %get-tuple-element.5), kind=kOutput, calls=%fused_computation.2 | convolution fusion | flops 1074790400 | bytes 6815744 | tf_op jit(solution)/shard_map/dot_general | solution.py:39
  86.7 0.1 fusion.32
  86.9 5.5 %collective-permute-start.16 = (bf16[2,64,512]{2,1,0:T(8,128)(2,1)S(1)}, bf16[2,64,512]{2,1,0:T(8,128)(2,1)S(1)}, u32[]{:S(2)}, u32[]{:S(2)}) collective-permute-start(bf16[2,64,512]{2,1,0:T(8,128)(2,1)S(1)} %get-tuple-element.25), channel_id=1, source_target_pairs={{0,32},{1,33},{4,36},{5,37},{8,40},{9,41},{12,44},{13,45},{16,48},... | collective-permute-start | bytes 393224 | tf_op jit(solution)/shard_map/ppermute | solution.py:61
  92.5 0.7 collective-permute-start.18
  93.1 1.3 %collective-permute-start.20 = (bf16[2,20,512]{2,1,0:T(8,128)(2,1)S(1)}, bf16[2,20,512]{2,1,0:T(8,128)(2,1)S(1)}, u32[]{:S(2)}, u32[]{:S(2)}) collective-permute-start(bf16[2,20,512]{2,1,0:T(8,128)(2,1)S(1)} %get-tuple-element.28), channel_id=1, source_target_pairs={{3,0},{7,4},{11,8},{15,12},{19,16},{23,20},{27,24},{35,32},{39,36}... | collective-permute-start | bytes 122888 | tf_op jit(solution)/shard_map/ppermute | solution.py:80
  94.4 1.3 %collective-permute-start.17 = (bf16[2,24,512]{2,1,0:T(8,128)(2,1)S(1)}, bf16[2,24,512]{2,1,0:T(8,128)(2,1)S(1)}, u32[]{:S(2)}, u32[]{:S(2)}) collective-permute-start(bf16[2,24,512]{2,1,0:T(8,128)(2,1)S(1)} %fusion.58), channel_id=1, source_target_pairs={{3,4},{7,8},{11,12},{15,16},{19,20},{23,24},{27,28},{35,36},{39,40... | collective-permute-start | bytes 147464 | tf_op jit(solution)/shard_map/ppermute | solution.py:85
  95.8 1.3 %collective-permute-start.19 = (bf16[2,20,512]{2,1,0:T(8,128)(2,1)S(1)}, bf16[2,20,512]{2,1,0:T(8,128)(2,1)S(1)}, u32[]{:S(2)}, u32[]{:S(2)}) collective-permute-start(bf16[2,20,512]{2,1,0:T(8,128)(2,1)S(1)} %collective-permute-done.18), channel_id=1, source_target_pairs={{1,4},{5,8},{9,12},{13,16},{17,20},{21,24},{25,28},{33,36},{37,40}... | collective-permute-start | bytes 122888 | tf_op jit(solution)/shard_map/ppermute | solution.py:85
  97.1 2.1 %collective-permute-done.20 = bf16[2,20,512]{2,1,0:T(8,128)(2,1)S(1)} collective-permute-done((bf16[2,20,512]{2,1,0:T(8,128)(2,1)S(1)}, bf16[2,20,512]{2,1,0:T(8,128)(2,1)S(1)}, u32[]{:S(2)}, u32[]{:S(2)}) %collective-permute-start.20) | collective-permute-done | bytes 40992 | tf_op jit(solution)/shard_map/ppermute | solution.py:80
  99.2 1.9 %collective-permute-start.21 = (bf16[2,20,512]{2,1,0:T(8,128)(2,1)S(1)}, bf16[2,20,512]{2,1,0:T(8,128)(2,1)S(1)}, u32[]{:S(2)}, u32[]{:S(2)}) collective-permute-start(bf16[2,20,512]{2,1,0:T(8,128)(2,1)S(1)} %collective-permute-done.20), channel_id=1, source_target_pairs={{0,4},{4,8},{8,12},{12,16},{16,20},{20,24},{24,28},{32,36},{36,40}... | collective-permute-start | bytes 122888 | tf_op jit(solution)/shard_map/ppermute | solution.py:85
  101.1 1.3 %collective-permute-start.22 = (bf16[2,64,512]{2,1,0:T(8,128)(2,1)S(1)}, bf16[2,64,512]{2,1,0:T(8,128)(2,1)S(1)}, u32[]{:S(2)}, u32[]{:S(2)}) collective-permute-start(bf16[2,64,512]{2,1,0:T(8,128)(2,1)S(1)} %get-tuple-element.26), channel_id=1, source_target_pairs={{0,1},{1,2},{4,5},{5,6},{8,9},{9,10},{12,13},{13,14},{16,17},{17,1... | collective-permute-start | bytes 393224 | tf_op jit(solution)/shard_map/ppermute | solution.py:65
  102.4 8.6 %collective-permute-done.17 = bf16[2,24,512]{2,1,0:T(8,128)(2,1)S(1)} collective-permute-done((bf16[2,24,512]{2,1,0:T(8,128)(2,1)S(1)}, bf16[2,24,512]{2,1,0:T(8,128)(2,1)S(1)}, u32[]{:S(2)}, u32[]{:S(2)}) %collective-permute-start.17) | collective-permute-done | bytes 49184 | tf_op jit(solution)/shard_map/ppermute | solution.py:85
  111.0 0.1 collective-permute-done.19
  111.1 2.6 %collective-permute-done.21 = bf16[2,20,512]{2,1,0:T(8,128)(2,1)S(1)} collective-permute-done((bf16[2,20,512]{2,1,0:T(8,128)(2,1)S(1)}, bf16[2,20,512]{2,1,0:T(8,128)(2,1)S(1)}, u32[]{:S(2)}, u32[]{:S(2)}) %collective-permute-start.21) | collective-permute-done | bytes 40992 | tf_op jit(solution)/shard_map/ppermute | solution.py:85
  113.8 0.1 fusion.46
  113.9 1.5 %fusion = f32[2,64,2,1024]{3,1,2,0:T(8,128)S(1)} fusion(bf16[1,1,2,1024,1024]{4,3,2,1,0:T(8,128)(2,1)S(1)} %copy-done.2, bf16[1,64,1024]{2,1,0:T(8,128)(2,1)S(1)} %get-tuple-element.20, bf16[1,64,1024]{2,1,0:T(8,128)(2,1)S(1)} %get-tuple-element.19), kind=kOutput, calls=%fused_computation | convolution fusion | flops 537395200 | bytes 5505024 | tf_op jit(solution)/shard_map/dot_general | solution.py:39
  115.4 0.1 fusion.49
  115.5 0.2 fusion.35
  115.7 1.1 copy.6
  (35 shorter events, 0.5 us)
Async XLA Ops:
  0.8 11.4 %copy-start.3 = (f32[3,2]{0,1:T(2,128)S(1)}, f32[3,2]{0,1:T(2,128)}, u32[]{:S(2)}) copy-start(f32[3,2]{0,1:T(2,128)} %param.9) | copy-start | bytes 76
  0.8 12.0 %copy-start.4 = (s32[1,1,1024]{2,1,0:T(1,128)S(1)}, s32[1,1,1024]{2,1,0:T(1,128)}, u32[]{:S(2)}) copy-start(s32[1,1,1024]{2,1,0:T(1,128)} %param.6) | copy-start | bytes 12292
  0.8 15.7 %copy-start.5 = (f32[1,1,2,128]{3,2,1,0:T(2,128)S(1)}, f32[1,1,2,128]{3,2,1,0:T(2,128)}, u32[]{:S(2)}) copy-start(f32[1,1,2,128]{3,2,1,0:T(2,128)} %param.8) | copy-start | bytes 3076
  4.3 13.0 %copy-start = (bf16[1,1,2,1024,1024]{4,3,2,1,0:T(8,128)(2,1)S(1)}, bf16[1,1,2,1024,1024]{4,3,2,1,0:T(8,128)(2,1)}, u32[]{:S(2)}) copy-start(bf16[1,1,2,1024,1024]{4,3,2,1,0:T(8,128)(2,1)} %param.5) | copy-start | bytes 12582916
  4.6 12.2 %collective-permute-start = (bf16[2,128,512]{2,1,0:T(8,128)(2,1)S(1)}, bf16[2,128,512]{2,1,0:T(8,128)(2,1)S(1)}, u32[]{:S(2)}, u32[]{:S(2)}) collective-permute-start(bf16[2,128,512]{2,1,0:T(8,128)(2,1)S(1)} %get-tuple-element.37), channel_id=1, source_target_pairs={{0,32},{1,33},{2,34},{3,35},{4,36},{5,37},{6,38},{7,39},{8,40},{9,... | collective-permute-start | bytes 786440 | tf_op jit(solution)/shard_map/ppermute | solution.py:61
  8.9 8.1 %collective-permute-start.1 = (bf16[2,128,512]{2,1,0:T(8,128)(2,1)S(1)}, bf16[2,128,512]{2,1,0:T(8,128)(2,1)S(1)}, u32[]{:S(2)}, u32[]{:S(2)}) collective-permute-start(bf16[2,128,512]{2,1,0:T(8,128)(2,1)S(1)} %get-tuple-element.38), channel_id=1, source_target_pairs={{0,1},{1,2},{2,3},{4,5},{5,6},{6,7},{8,9},{9,10},{10,11},{12,13},{... | collective-permute-start | bytes 786440 | tf_op jit(solution)/shard_map/ppermute | solution.py:65
  18.9 22.3 %collective-permute-start.2 = (bf16[2,128,512]{2,1,0:T(8,128)(2,1)S(1)}, bf16[2,128,512]{2,1,0:T(8,128)(2,1)S(1)}, u32[]{:S(2)}, u32[]{:S(2)}) collective-permute-start(bf16[2,128,512]{2,1,0:T(8,128)(2,1)S(1)} %get-tuple-element.33), channel_id=1, source_target_pairs={{1,33},{2,34},{3,35},{5,37},{6,38},{7,39},{9,41},{10,42},{11,43},{... | collective-permute-start | bytes 786440 | tf_op jit(solution)/shard_map/ppermute | solution.py:61
  19.6 4.6 %collective-permute-start.4 = (bf16[2,40,512]{2,1,0:T(8,128)(2,1)S(1)}, bf16[2,40,512]{2,1,0:T(8,128)(2,1)}, u32[]{:S(2)}, u32[]{:S(2)}) collective-permute-start(bf16[2,40,512]{2,1,0:T(8,128)(2,1)S(1)} %get-tuple-element.35), channel_id=1, source_target_pairs={{3,1},{7,5},{11,9},{15,13},{19,17},{23,21},{27,25},{35,33},{39,37}... | collective-permute-start | bytes 245768 | tf_op jit(solution)/shard_map/ppermute | solution.py:80
  20.9 11.8 %collective-permute-start.6 = (bf16[2,40,512]{2,1,0:T(8,128)(2,1)S(1)}, bf16[2,40,512]{2,1,0:T(8,128)(2,1)}, u32[]{:S(2)}, u32[]{:S(2)}) collective-permute-start(bf16[2,40,512]{2,1,0:T(8,128)(2,1)S(1)} %get-tuple-element.36), channel_id=1, source_target_pairs={{3,0},{7,4},{11,8},{15,12},{19,16},{23,20},{27,24},{35,32},{39,36}... | collective-permute-start | bytes 245768 | tf_op jit(solution)/shard_map/ppermute | solution.py:80
  22.2 32.8 %collective-permute-start.8 = (bf16[2,128,512]{2,1,0:T(8,128)(2,1)S(1)}, bf16[2,128,512]{2,1,0:T(8,128)(2,1)S(1)}, u32[]{:S(2)}, u32[]{:S(2)}) collective-permute-start(bf16[2,128,512]{2,1,0:T(8,128)(2,1)S(1)} %get-tuple-element.34), channel_id=1, source_target_pairs={{1,2},{2,3},{5,6},{6,7},{9,10},{10,11},{13,14},{14,15},{17,18},{18... | collective-permute-start | bytes 786440 | tf_op jit(solution)/shard_map/ppermute | solution.py:65
  22.9 32.1 %collective-permute-start.3 = (bf16[2,48,512]{2,1,0:T(8,128)(2,1)S(1)}, bf16[2,48,512]{2,1,0:T(8,128)(2,1)S(1)}, u32[]{:S(2)}, u32[]{:S(2)}) collective-permute-start(bf16[2,48,512]{2,1,0:T(8,128)(2,1)S(1)} %fusion.54), channel_id=1, source_target_pairs={{3,4},{7,8},{11,12},{15,16},{19,20},{23,24},{27,28},{35,36},{39,40... | collective-permute-start | bytes 294920 | tf_op jit(solution)/shard_map/ppermute | solution.py:85
  24.2 31.2 %copy-start.1 = (bf16[1,1,2,1024,1024]{4,3,2,1,0:T(8,128)(2,1)S(1)}, bf16[1,1,2,1024,1024]{4,3,2,1,0:T(8,128)(2,1)}, u32[]{:S(2)}) copy-start(bf16[1,1,2,1024,1024]{4,3,2,1,0:T(8,128)(2,1)} %param.5) | copy-start | bytes 12582916
  24.2 30.7 %collective-permute-start.5 = (bf16[2,40,512]{2,1,0:T(8,128)(2,1)}, bf16[2,40,512]{2,1,0:T(8,128)(2,1)S(1)}, u32[]{:S(2)}, u32[]{:S(2)}) collective-permute-start(bf16[2,40,512]{2,1,0:T(8,128)(2,1)} %collective-permute-done.4), channel_id=1, source_target_pairs={{1,4},{5,8},{9,12},{13,16},{17,20},{21,24},{25,28},{33,36},{37,40}... | collective-permute-start | bytes 245768 | tf_op jit(solution)/shard_map/ppermute | solution.py:85
  32.7 22.3 %collective-permute-start.7 = (bf16[2,40,512]{2,1,0:T(8,128)(2,1)}, bf16[2,40,512]{2,1,0:T(8,128)(2,1)S(1)}, u32[]{:S(2)}, u32[]{:S(2)}) collective-permute-start(bf16[2,40,512]{2,1,0:T(8,128)(2,1)} %collective-permute-done.6), channel_id=1, source_target_pairs={{0,4},{4,8},{8,12},{12,16},{16,20},{20,24},{24,28},{32,36},{36,40}... | collective-permute-start | bytes 245768 | tf_op jit(solution)/shard_map/ppermute | solution.py:85
  56.9 15.4 %collective-permute-start.9 = (bf16[2,128,512]{2,1,0:T(8,128)(2,1)S(1)}, bf16[2,128,512]{2,1,0:T(8,128)(2,1)S(1)}, u32[]{:S(2)}, u32[]{:S(2)}) collective-permute-start(bf16[2,128,512]{2,1,0:T(8,128)(2,1)S(1)} %get-tuple-element.29), channel_id=1, source_target_pairs={{0,32},{2,34},{3,35},{4,36},{6,38},{7,39},{8,40},{10,42},{11,43},{... | collective-permute-start | bytes 786440 | tf_op jit(solution)/shard_map/ppermute | solution.py:61
  60.4 25.0 %copy-start.2 = (bf16[1,1,2,1024,1024]{4,3,2,1,0:T(8,128)(2,1)S(1)}, bf16[1,1,2,1024,1024]{4,3,2,1,0:T(8,128)(2,1)}, u32[]{:S(2)}) copy-start(bf16[1,1,2,1024,1024]{4,3,2,1,0:T(8,128)(2,1)} %param.5) | copy-start | bytes 12582916
  60.4 4.9 %collective-permute-start.11 = (bf16[2,40,512]{2,1,0:T(8,128)(2,1)S(1)}, bf16[2,40,512]{2,1,0:T(8,128)(2,1)S(1)}, u32[]{:S(2)}, u32[]{:S(2)}) collective-permute-start(bf16[2,40,512]{2,1,0:T(8,128)(2,1)S(1)} %get-tuple-element.31), channel_id=1, source_target_pairs={{3,1},{7,5},{11,9},{15,13},{19,17},{23,21},{27,25},{35,33},{39,37}... | collective-permute-start | bytes 245768 | tf_op jit(solution)/shard_map/ppermute | solution.py:80
  61.3 6.8 %collective-permute-start.13 = (bf16[2,40,512]{2,1,0:T(8,128)(2,1)S(1)}, bf16[2,40,512]{2,1,0:T(8,128)(2,1)S(1)}, u32[]{:S(2)}, u32[]{:S(2)}) collective-permute-start(bf16[2,40,512]{2,1,0:T(8,128)(2,1)S(1)} %get-tuple-element.32), channel_id=1, source_target_pairs={{3,0},{7,4},{11,8},{15,12},{19,16},{23,20},{27,24},{35,32},{39,36}... | collective-permute-start | bytes 245768 | tf_op jit(solution)/shard_map/ppermute | solution.py:80
  62.7 22.3 %collective-permute-start.15 = (bf16[2,128,512]{2,1,0:T(8,128)(2,1)S(1)}, bf16[2,128,512]{2,1,0:T(8,128)(2,1)S(1)}, u32[]{:S(2)}, u32[]{:S(2)}) collective-permute-start(bf16[2,128,512]{2,1,0:T(8,128)(2,1)S(1)} %get-tuple-element.30), channel_id=1, source_target_pairs={{0,1},{2,3},{4,5},{6,7},{8,9},{10,11},{12,13},{14,15},{16,17},{18,... | collective-permute-start | bytes 786440 | tf_op jit(solution)/shard_map/ppermute | solution.py:65
  64.0 20.8 %collective-permute-start.10 = (bf16[2,48,512]{2,1,0:T(8,128)(2,1)S(1)}, bf16[2,48,512]{2,1,0:T(8,128)(2,1)S(1)}, u32[]{:S(2)}, u32[]{:S(2)}) collective-permute-start(bf16[2,48,512]{2,1,0:T(8,128)(2,1)S(1)} %fusion.53), channel_id=1, source_target_pairs={{3,4},{7,8},{11,12},{15,16},{19,20},{23,24},{27,28},{35,36},{39,40... | collective-permute-start | bytes 294920 | tf_op jit(solution)/shard_map/ppermute | solution.py:85
  65.3 19.5 %collective-permute-start.12 = (bf16[2,40,512]{2,1,0:T(8,128)(2,1)S(1)}, bf16[2,40,512]{2,1,0:T(8,128)(2,1)S(1)}, u32[]{:S(2)}, u32[]{:S(2)}) collective-permute-start(bf16[2,40,512]{2,1,0:T(8,128)(2,1)S(1)} %collective-permute-done.11), channel_id=1, source_target_pairs={{1,4},{5,8},{9,12},{13,16},{17,20},{21,24},{25,28},{33,36},{37,40}... | collective-permute-start | bytes 245768 | tf_op jit(solution)/shard_map/ppermute | solution.py:85
  68.1 16.9 %collective-permute-start.14 = (bf16[2,40,512]{2,1,0:T(8,128)(2,1)S(1)}, bf16[2,40,512]{2,1,0:T(8,128)(2,1)S(1)}, u32[]{:S(2)}, u32[]{:S(2)}) collective-permute-start(bf16[2,40,512]{2,1,0:T(8,128)(2,1)S(1)} %collective-permute-done.13), channel_id=1, source_target_pairs={{0,4},{4,8},{8,12},{12,16},{16,20},{20,24},{24,28},{32,36},{36,40}... | collective-permute-start | bytes 245768 | tf_op jit(solution)/shard_map/ppermute | solution.py:85
  86.9 15.5 %collective-permute-start.16 = (bf16[2,64,512]{2,1,0:T(8,128)(2,1)S(1)}, bf16[2,64,512]{2,1,0:T(8,128)(2,1)S(1)}, u32[]{:S(2)}, u32[]{:S(2)}) collective-permute-start(bf16[2,64,512]{2,1,0:T(8,128)(2,1)S(1)} %get-tuple-element.25), channel_id=1, source_target_pairs={{0,32},{1,33},{4,36},{5,37},{8,40},{9,41},{12,44},{13,45},{16,48},... | collective-permute-start | bytes 393224 | tf_op jit(solution)/shard_map/ppermute | solution.py:61
  92.5 3.3 %collective-permute-start.18 = (bf16[2,20,512]{2,1,0:T(8,128)(2,1)S(1)}, bf16[2,20,512]{2,1,0:T(8,128)(2,1)S(1)}, u32[]{:S(2)}, u32[]{:S(2)}) collective-permute-start(bf16[2,20,512]{2,1,0:T(8,128)(2,1)S(1)} %get-tuple-element.27), channel_id=1, source_target_pairs={{3,1},{7,5},{11,9},{15,13},{19,17},{23,21},{27,25},{35,33},{39,37}... | collective-permute-start | bytes 122888 | tf_op jit(solution)/shard_map/ppermute | solution.py:80
  93.1 6.0 %collective-permute-start.20 = (bf16[2,20,512]{2,1,0:T(8,128)(2,1)S(1)}, bf16[2,20,512]{2,1,0:T(8,128)(2,1)S(1)}, u32[]{:S(2)}, u32[]{:S(2)}) collective-permute-start(bf16[2,20,512]{2,1,0:T(8,128)(2,1)S(1)} %get-tuple-element.28), channel_id=1, source_target_pairs={{3,0},{7,4},{11,8},{15,12},{19,16},{23,20},{27,24},{35,32},{39,36}... | collective-permute-start | bytes 122888 | tf_op jit(solution)/shard_map/ppermute | solution.py:80
  94.4 16.6 %collective-permute-start.17 = (bf16[2,24,512]{2,1,0:T(8,128)(2,1)S(1)}, bf16[2,24,512]{2,1,0:T(8,128)(2,1)S(1)}, u32[]{:S(2)}, u32[]{:S(2)}) collective-permute-start(bf16[2,24,512]{2,1,0:T(8,128)(2,1)S(1)} %fusion.58), channel_id=1, source_target_pairs={{3,4},{7,8},{11,12},{15,16},{19,20},{23,24},{27,28},{35,36},{39,40... | collective-permute-start | bytes 147464 | tf_op jit(solution)/shard_map/ppermute | solution.py:85
  95.8 15.4 %collective-permute-start.19 = (bf16[2,20,512]{2,1,0:T(8,128)(2,1)S(1)}, bf16[2,20,512]{2,1,0:T(8,128)(2,1)S(1)}, u32[]{:S(2)}, u32[]{:S(2)}) collective-permute-start(bf16[2,20,512]{2,1,0:T(8,128)(2,1)S(1)} %collective-permute-done.18), channel_id=1, source_target_pairs={{1,4},{5,8},{9,12},{13,16},{17,20},{21,24},{25,28},{33,36},{37,40}... | collective-permute-start | bytes 122888 | tf_op jit(solution)/shard_map/ppermute | solution.py:85
  99.2 14.5 %collective-permute-start.21 = (bf16[2,20,512]{2,1,0:T(8,128)(2,1)S(1)}, bf16[2,20,512]{2,1,0:T(8,128)(2,1)S(1)}, u32[]{:S(2)}, u32[]{:S(2)}) collective-permute-start(bf16[2,20,512]{2,1,0:T(8,128)(2,1)S(1)} %collective-permute-done.20), channel_id=1, source_target_pairs={{0,4},{4,8},{8,12},{12,16},{16,20},{20,24},{24,28},{32,36},{36,40}... | collective-permute-start | bytes 122888 | tf_op jit(solution)/shard_map/ppermute | solution.py:85
  101.1 12.6 %collective-permute-start.22 = (bf16[2,64,512]{2,1,0:T(8,128)(2,1)S(1)}, bf16[2,64,512]{2,1,0:T(8,128)(2,1)S(1)}, u32[]{:S(2)}, u32[]{:S(2)}) collective-permute-start(bf16[2,64,512]{2,1,0:T(8,128)(2,1)S(1)} %get-tuple-element.26), channel_id=1, source_target_pairs={{0,1},{1,2},{4,5},{5,6},{8,9},{9,10},{12,13},{13,14},{16,17},{17,1... | collective-permute-start | bytes 393224 | tf_op jit(solution)/shard_map/ppermute | solution.py:65

commit v2 on v1

--- a/solution.py
+++ b/solution.py
@@ -1,12 +1,17 @@
 import jax
 import jax.numpy as jnp
 from jax import lax
+from jax.experimental import pallas as pl
 from jax.sharding import PartitionSpec as P
 
 
 NB = 64
 BLOCK = 4
-PIECES = ((3, 48), (1, 40), (0, 40))
+PIECES = ((3, 48), (1, 40), (2, 40))
+
+
+def copy_kernel(source_ref, target_ref):
+    target_ref[...] = source_ref[...]
 
 
 def per_device(green_ops, cell_map, dipole_site, dipole_amp, contrast):
@@ -25,13 +30,8 @@
     hot = lax.broadcasted_iota(jnp.int32, (width, rows), 1) == sites[:, None]
     source = jnp.where(hot[None], amplitude[:, :, None], 0.0)
 
-    def factor_of(part):
-        return jnp.where(
-            cells == 0, contrast[0, part], jnp.where(cells == 1, contrast[1, part], contrast[2, part])
-        )
-
-    real_factor = factor_of(0)
-    imag_factor = factor_of(1)
+    classes = lax.broadcasted_iota(jnp.int32, (contrast.shape[0], 1, rows), 0)
+    factor = jnp.where(classes == cells[None], contrast[:, :, None], 0.0).sum(axis=0)
 
     def apply(excited):
         live = excited.shape[1]
@@ -45,6 +45,7 @@
         return jnp.stack([real_out, imag_out]).astype(jnp.bfloat16)
 
     def step(west, south):
+        real_factor, imag_factor = factor[0:1], factor[1:2]
         incoming = jnp.concatenate([west, south], axis=2).astype(jnp.float32)
         live = incoming.shape[1]
         real_in = real_factor * incoming[0] - imag_factor * incoming[1] + source[0, :live]
@@ -95,20 +96,23 @@
     s2 = north_to(t1, (1, 2))
     x2 = cross(t1)
 
-    t2 = step(jnp.where(lane == 0, w1, w2), jnp.where(lane == 0, x1, s2))
-    w3 = east_to(t2, (0, 2, 3))
-    s3 = north_to(t2, (0, 2))
+    t2 = step(w2, s2)
     x3 = cross(t2[:, :NB])
 
-    t3 = step(jnp.where(lane == 1, w2, w3), jnp.where(lane == 0, x2, s3))
-    w4 = east_to(t3[:, :NB], (0, 1))
-    s4 = north_to(t3[:, :NB], (0, 1))
+    factor = pl.pallas_call(copy_kernel, out_shape=jax.ShapeDtypeStruct(factor.shape, factor.dtype))(factor)
+    w1, x1, t2 = lax.optimization_barrier((w1, x1, t2))
+    late1 = step(w1, x1)
+    w3 = east_to(late1, (0,))
+    s3 = north_to(late1, (0,))
 
-    t4 = step(jnp.where(lane == 2, w3[:, :NB], w4), jnp.where(lane == 0, x3, s4))
+    late2 = step(jnp.where(lane == 0, w3, w2), jnp.where(lane == 0, x2, s3))
+    after_two = jnp.where(lane >= 2, t2, late2)
+    first = after_two[:, :NB]
+    w4 = east_to(first, (0, 1, 2, 3))
+    s4 = north_to(first, (0, 1, 2))
 
-    first = jnp.where(lane == 3, t3[:, :NB], t4)
-    second = jnp.where(lane >= 2, t2[:, NB:], t3[:, NB:])
-    traces = jnp.concatenate([first, second], axis=1)
+    t3 = step(w4, jnp.where(lane == 0, x3, s4))
+    traces = jnp.concatenate([t3, after_two[:, NB:]], axis=1)
     return traces.transpose(2, 0, 1)[None, None]
 
 

time: 118 us -> 103 us (0.87)
  waiting for transfers between devices: 48.4 us -> 29.1 us
  starting transfers between devices: 49.9 us -> 54.3 us
  other arithmetic: 7.17 us -> 3.82 us
  matrix products: 8.89 us -> 10.2 us
  Pallas kernels: 0 us -> 1.29 us
    ppermute x4, starting transfers between devices: 6.5 us -> 24.2 us  [north_to(): return lax.ppermute(traces[:, :, face:], 'gy', pairs)]
    ppermute x9, waiting for transfers between devices: 37.6 us -> 26.8 us  [cross(): arrived.append(lax.ppermute(piece, 'gy', pairs))]
    ppermute x9, starting transfers between devices: 22.6 us -> 11.9 us  [cross(): arrived.append(lax.ppermute(piece, 'gy', pairs))]
    ppermute x6, waiting for transfers between devices: 10.5 us -> 0.02 us  [cross(): piece = lax.ppermute(piece, 'gy', pairs)]
    select_n x8 -> x4, other arithmetic: 4.17 us -> 0.21 us  [the longest x2 0.1 us: per_device(): late2 = step(jnp.where(lane == 0, w3, w2), jnp.where(lane == 0, x2, s3))]
    ppermute x6, starting transfers between devices: 6.75 us -> 3.99 us  [cross(): piece = lax.ppermute(piece, 'gy', pairs)]
    ppermute x4, waiting for transfers between devices: 0.3 us -> 2.26 us  [north_to(): return lax.ppermute(traces[:, :, face:], 'gy', pairs)]
    dot_general x5 -> x6, matrix products: 8.89 us -> 10.2 us  [apply(): lax.dot_general(flat, operator, (((1,), (2,)), ((), ())), preferred_eleme...]
  transfers between devices with their start and end apart: 23 -> 23, of which waited for: 10 -> 6; matrix products, arithmetic and copies ran while one was open for 4% -> 4% of each run, Pallas kernels for 0% -> 1%
where the time goes in v2:
time: 103 us; the launch traced here: 101 us
  starting transfers between devices  54.3 us (53%)
  waiting for transfers between devices  29.1 us (28%)
  matrix products  10.2 us (10%)
  other arithmetic  3.82 us (4%)
  local copies, waits for them, and re-layouts  1.87 us (2%)
  Pallas kernels  1.29 us (1%)
    ppermute x9, waiting for transfers between devices, cross(): arrived.append(lax.ppermute(piece, 'gy', pairs))  26.8 us
    ppermute x4, starting transfers between devices, north_to(): return lax.ppermute(traces[:, :, face:], 'gy', pairs)  24.2 us
    ppermute x4, starting transfers between devices, east_to(): return lax.ppermute(traces[:, :, :face], ('gx', 'gy'), pairs)  14.2 us
    ppermute x9, starting transfers between devices, cross(): arrived.append(lax.ppermute(piece, 'gy', pairs))  11.9 us
    dot_general x6, matrix products, apply(): lax.dot_general(flat, operator, (((1,), (2,)), ((), ())), preferred_eleme...  10.2 us
    ppermute x6, starting transfers between devices, cross(): piece = lax.ppermute(piece, 'gy', pairs)  3.99 us
    ppermute x4, waiting for transfers between devices, north_to(): return lax.ppermute(traces[:, :, face:], 'gy', pairs)  2.26 us
  transfers between devices with their start and end apart: 23, of which 6 were waited for; matrix products, arithmetic and copies ran while one was open for 4% of the time, Pallas kernels for 1%

profile of v2, /device:TPU:7, one launch (start us, length us, event | category | flops | bytes accessed | tf_op | source)
XLA Modules:
  0.0 101.3 jit_solution(9854333291037094780)
XLA Ops:
  0.0 0.8 iota_compare_fusion
  0.8 3.5 %fusion.10 = f32[2,128,2,1024]{3,1,2,0:T(8,128)S(1)} fusion(bf16[1,1,2,1024,1024]{4,3,2,1,0:T(8,128)(2,1)} %param.5, f32[2,128]{1,0:T(2,128)} %bitcast.91, pred[128,1024]{1,0:T(8,128)(4,1)S(1)} %iota_compare_fusion), kind=kOutput, calls=%fused_computation.10 | convolution fusion | flops 1074003968 | bytes 6423552 | tf_op jit(solution)/shard_map/dot_general | solution.py:39
  4.3 0.0 copy-start.6
  4.3 0.0 copy-start.5
  4.3 0.0 copy-start.4
  4.3 0.1 fusion.34
  4.5 1.3 %collective-permute-start.1 = (bf16[2,48,512]{2,1,0:T(8,128)(2,1)S(1)}, bf16[2,48,512]{2,1,0:T(8,128)(2,1)S(1)}, u32[]{:S(2)}, u32[]{:S(2)}) collective-permute-start(bf16[2,48,512]{2,1,0:T(8,128)(2,1)S(1)} %fusion.55), channel_id=1, source_target_pairs={{3,4},{7,8},{11,12},{15,16},{19,20},{23,24},{27,28},{35,36},{39,40... | collective-permute-start | bytes 294920 | tf_op jit(solution)/shard_map/ppermute | solution.py:86
  5.8 0.7 collective-permute-start.2
  6.5 0.7 collective-permute-start.4
  7.2 3.2 %collective-permute-start.6 = (bf16[2,128,512]{2,1,0:T(8,128)(2,1)S(1)}, bf16[2,128,512]{2,1,0:T(8,128)(2,1)S(1)}, u32[]{:S(2)}, u32[]{:S(2)}) collective-permute-start(bf16[2,128,512]{2,1,0:T(8,128)(2,1)S(1)} %get-tuple-element.43), channel_id=1, source_target_pairs={{0,1},{1,2},{2,3},{4,5},{5,6},{6,7},{8,9},{9,10},{10,11},{12,13},{... | collective-permute-start | bytes 786440 | tf_op jit(solution)/shard_map/ppermute | solution.py:66
  10.4 4.4 %collective-permute-start = (bf16[2,128,512]{2,1,0:T(8,128)(2,1)S(1)}, bf16[2,128,512]{2,1,0:T(8,128)(2,1)S(1)}, u32[]{:S(2)}, u32[]{:S(2)}) collective-permute-start(bf16[2,128,512]{2,1,0:T(8,128)(2,1)S(1)} %get-tuple-element.44), channel_id=1, source_target_pairs={{0,32},{1,33},{2,34},{3,35},{4,36},{5,37},{6,38},{7,39},{8,40},{9,... | collective-permute-start | bytes 786440 | tf_op jit(solution)/shard_map/ppermute | solution.py:62
  14.8 0.2 broadcast_select_fusion
  15.0 0.1 copy.8
  15.1 0.1 select_reduce_fusion.source_ref
  15.2 0.0 copy-start.2
  15.2 0.6 copy-done.2
  15.8 1.3 %shard_map.55 = f32[2,1024]{1,0:T(2,128)} custom-call(f32[2,1024]{1,0:T(2,128)} %copy-done.2), custom_call_target="tpu_custom_call" | custom-call | tf_op jit(solution)/shard_map/pallas_call | solution.py:102
  17.1 1.5 %collective-permute-start.3 = (bf16[2,40,512]{2,1,0:T(8,128)(2,1)S(1)}, bf16[2,40,512]{2,1,0:T(8,128)(2,1)S(1)}, u32[]{:S(2)}, u32[]{:S(2)}) collective-permute-start(bf16[2,40,512]{2,1,0:T(8,128)(2,1)S(1)} %collective-permute-done.2), channel_id=1, source_target_pairs={{1,4},{5,8},{9,12},{13,16},{17,20},{21,24},{25,28},{33,36},{37,40}... | collective-permute-start | bytes 245768 | tf_op jit(solution)/shard_map/ppermute | solution.py:86
  18.7 1.3 %collective-permute-start.5 = (bf16[2,40,512]{2,1,0:T(8,128)(2,1)S(1)}, bf16[2,40,512]{2,1,0:T(8,128)(2,1)S(1)}, u32[]{:S(2)}, u32[]{:S(2)}) collective-permute-start(bf16[2,40,512]{2,1,0:T(8,128)(2,1)S(1)} %collective-permute-done.4), channel_id=1, source_target_pairs={{2,4},{6,8},{10,12},{14,16},{18,20},{22,24},{26,28},{34,36},{38,40... | collective-permute-start | bytes 245768 | tf_op jit(solution)/shard_map/ppermute | solution.py:86
  20.0 0.1 maximum_convert_fusion
  20.1 0.2 add_convert_fusion.7
  20.4 1.3 %fusion.8 = f32[2,128,2,1024]{3,1,2,0:T(8,128)S(1)} fusion(bf16[1,1,2,1024,1024]{4,3,2,1,0:T(8,128)(2,1)S(1)} %copy-done, bf16[1,128,1024]{2,1,0:T(8,128)(2,1)S(1)} %get-tuple-element.18, bf16[1,128,1024]{2,1,0:T(8,128)(2,1)S(1)} %get-tuple-element.17), kind=kOutput, calls=%fused_computation.8 | convolution fusion | flops 1074790400 | bytes 6815744 | tf_op jit(solution)/shard_map/dot_general | solution.py:39
  21.7 0.1 fusion.36
  21.9 0.7 collective-permute-start.7
  22.6 0.7 collective-permute-start.8
  23.3 1.2 %collective-permute-done.1 = bf16[2,48,512]{2,1,0:T(8,128)(2,1)S(1)} collective-permute-done((bf16[2,48,512]{2,1,0:T(8,128)(2,1)S(1)}, bf16[2,48,512]{2,1,0:T(8,128)(2,1)S(1)}, u32[]{:S(2)}, u32[]{:S(2)}) %collective-permute-start.1) | collective-permute-done | bytes 98336 | tf_op jit(solution)/shard_map/ppermute | solution.py:86
  24.5 10.1 %collective-permute-done.3 = bf16[2,40,512]{2,1,0:T(8,128)(2,1)S(1)} collective-permute-done((bf16[2,40,512]{2,1,0:T(8,128)(2,1)S(1)}, bf16[2,40,512]{2,1,0:T(8,128)(2,1)S(1)}, u32[]{:S(2)}, u32[]{:S(2)}) %collective-permute-start.3) | collective-permute-done | bytes 81952 | tf_op jit(solution)/shard_map/ppermute | solution.py:86
  34.6 4.4 %collective-permute-done.5 = bf16[2,40,512]{2,1,0:T(8,128)(2,1)S(1)} collective-permute-done((bf16[2,40,512]{2,1,0:T(8,128)(2,1)S(1)}, bf16[2,40,512]{2,1,0:T(8,128)(2,1)S(1)}, u32[]{:S(2)}, u32[]{:S(2)}) %collective-permute-start.5) | collective-permute-done | bytes 81952 | tf_op jit(solution)/shard_map/ppermute | solution.py:86
  39.1 0.1 maximum_convert_fusion.1
  39.2 0.2 add_convert_fusion.5
  39.5 1.3 %fusion.6 = f32[2,128,2,1024]{3,1,2,0:T(8,128)S(1)} fusion(bf16[1,1,2,1024,1024]{4,3,2,1,0:T(8,128)(2,1)S(1)} %copy-done.1, bf16[1,128,1024]{2,1,0:T(8,128)(2,1)S(1)} %get-tuple-element.16, bf16[1,128,1024]{2,1,0:T(8,128)(2,1)S(1)} %get-tuple-element.15), kind=kOutput, calls=%fused_computation.6 | convolution fusion | flops 1074790400 | bytes 6815744 | tf_op jit(solution)/shard_map/dot_general | solution.py:39
  40.8 0.1 fusion.37
  40.9 0.1 pad_maximum_fusion
  41.0 0.1 maximum_convert_fusion.2
  41.1 0.2 add_convert_fusion.3
  41.3 1.3 %fusion.4 = f32[2,128,2,1024]{3,1,2,0:T(8,128)S(1)} fusion(bf16[1,1,2,1024,1024]{4,3,2,1,0:T(8,128)(2,1)S(1)} %copy-done.1, bf16[1,128,1024]{2,1,0:T(8,128)(2,1)S(1)} %get-tuple-element.14, bf16[1,128,1024]{2,1,0:T(8,128)(2,1)S(1)} %get-tuple-element.13), kind=kOutput, calls=%fused_computation.4 | convolution fusion | flops 1074790400 | bytes 6815744 | tf_op jit(solution)/shard_map/dot_general | solution.py:39
  42.6 0.1 fusion.39
  42.8 4.1 %collective-permute-start.9 = (bf16[2,128,512]{2,1,0:T(8,128)(2,1)S(1)}, bf16[2,128,512]{2,1,0:T(8,128)(2,1)S(1)}, u32[]{:S(2)}, u32[]{:S(2)}) collective-permute-start(bf16[2,128,512]{2,1,0:T(8,128)(2,1)S(1)} %get-tuple-element.37), channel_id=1, source_target_pairs={{0,32},{4,36},{8,40},{12,44},{16,48},{20,52},{24,56},{28,60},{32,6... | collective-permute-start | bytes 786440 | tf_op jit(solution)/shard_map/ppermute | solution.py:62
  46.9 0.7 collective-permute-start.11
  47.6 0.7 collective-permute-start.13
  48.3 1.3 %collective-permute-start.10 = (bf16[2,48,512]{2,1,0:T(8,128)(2,1)S(1)}, bf16[2,48,512]{2,1,0:T(8,128)(2,1)S(1)}, u32[]{:S(2)}, u32[]{:S(2)}) collective-permute-start(bf16[2,48,512]{2,1,0:T(8,128)(2,1)S(1)} %fusion.54), channel_id=1, source_target_pairs={{3,4},{7,8},{11,12},{15,16},{19,20},{23,24},{27,28},{35,36},{39,40... | collective-permute-start | bytes 294920 | tf_op jit(solution)/shard_map/ppermute | solution.py:86
  49.6 1.3 %collective-permute-start.12 = (bf16[2,40,512]{2,1,0:T(8,128)(2,1)S(1)}, bf16[2,40,512]{2,1,0:T(8,128)(2,1)S(1)}, u32[]{:S(2)}, u32[]{:S(2)}) collective-permute-start(bf16[2,40,512]{2,1,0:T(8,128)(2,1)S(1)} %collective-permute-done.11), channel_id=1, source_target_pairs={{1,4},{5,8},{9,12},{13,16},{17,20},{21,24},{25,28},{33,36},{37,40}... | collective-permute-start | bytes 245768 | tf_op jit(solution)/shard_map/ppermute | solution.py:86
  50.9 1.3 %collective-permute-start.14 = (bf16[2,40,512]{2,1,0:T(8,128)(2,1)S(1)}, bf16[2,40,512]{2,1,0:T(8,128)(2,1)S(1)}, u32[]{:S(2)}, u32[]{:S(2)}) collective-permute-start(bf16[2,40,512]{2,1,0:T(8,128)(2,1)S(1)} %collective-permute-done.13), channel_id=1, source_target_pairs={{2,4},{6,8},{10,12},{14,16},{18,20},{22,24},{26,28},{34,36},{38,40... | collective-permute-start | bytes 245768 | tf_op jit(solution)/shard_map/ppermute | solution.py:86
  52.2 16.5 %collective-permute-start.15 = (bf16[2,128,512]{2,1,0:T(8,128)(2,1)S(1)}, bf16[2,128,512]{2,1,0:T(8,128)(2,1)S(1)}, u32[]{:S(2)}, u32[]{:S(2)}) collective-permute-start(bf16[2,128,512]{2,1,0:T(8,128)(2,1)S(1)} %get-tuple-element.38), channel_id=1, source_target_pairs={{0,1},{4,5},{8,9},{12,13},{16,17},{20,21},{24,25},{28,29},{32,33},... | collective-permute-start | bytes 786440 | tf_op jit(solution)/shard_map/ppermute | solution.py:66
  68.8 0.7 collective-permute-start.18
  69.5 0.7 collective-permute-start.20
  70.2 2.3 %collective-permute-done.15 = bf16[2,128,512]{2,1,0:T(8,128)(2,1)S(1)} collective-permute-done((bf16[2,128,512]{2,1,0:T(8,128)(2,1)S(1)}, bf16[2,128,512]{2,1,0:T(8,128)(2,1)S(1)}, u32[]{:S(2)}, u32[]{:S(2)}) %collective-permute-start.15) | collective-permute-done | bytes 262176 | tf_op jit(solution)/shard_map/ppermute | solution.py:66
  72.5 0.1 maximum_select_fusion.1
  72.6 0.1 maximum_convert_fusion.3
  72.7 0.2 add_convert_fusion.1
  72.9 1.3 %fusion.2 = f32[2,128,2,1024]{3,1,2,0:T(8,128)S(1)} fusion(bf16[1,1,2,1024,1024]{4,3,2,1,0:T(8,128)(2,1)S(1)} %copy-done.1, bf16[1,128,1024]{2,1,0:T(8,128)(2,1)S(1)} %get-tuple-element.12, bf16[1,128,1024]{2,1,0:T(8,128)(2,1)S(1)} %get-tuple-element.11), kind=kOutput, calls=%fused_computation.2 | convolution fusion | flops 1074790400 | bytes 6815744 | tf_op jit(solution)/shard_map/dot_general | solution.py:39
  74.2 0.1 fusion.41
  74.3 0.1 maximum_select_fusion
  74.5 3.8 %collective-permute-start.22 = (bf16[2,64,512]{2,1,0:T(8,128)(2,1)S(1)}, bf16[2,64,512]{2,1,0:T(8,128)(2,1)S(1)}, u32[]{:S(2)}, u32[]{:S(2)}) collective-permute-start(bf16[2,64,512]{2,1,0:T(8,128)(2,1)S(1)} %get-tuple-element.34), channel_id=1, source_target_pairs={{0,1},{1,2},{2,3},{4,5},{5,6},{6,7},{8,9},{9,10},{10,11},{12,13},{... | collective-permute-start | bytes 393224 | tf_op jit(solution)/shard_map/ppermute | solution.py:66
  78.3 1.3 %collective-permute-start.17 = (bf16[2,24,512]{2,1,0:T(8,128)(2,1)S(1)}, bf16[2,24,512]{2,1,0:T(8,128)(2,1)S(1)}, u32[]{:S(2)}, u32[]{:S(2)}) collective-permute-start(bf16[2,24,512]{2,1,0:T(8,128)(2,1)S(1)} %fusion.59), channel_id=1, source_target_pairs={{3,4},{7,8},{11,12},{15,16},{19,20},{23,24},{27,28},{35,36},{39,40... | collective-permute-start | bytes 147464 | tf_op jit(solution)/shard_map/ppermute | solution.py:86
  79.6 1.3 %collective-permute-start.19 = (bf16[2,20,512]{2,1,0:T(8,128)(2,1)S(1)}, bf16[2,20,512]{2,1,0:T(8,128)(2,1)S(1)}, u32[]{:S(2)}, u32[]{:S(2)}) collective-permute-start(bf16[2,20,512]{2,1,0:T(8,128)(2,1)S(1)} %collective-permute-done.18), channel_id=1, source_target_pairs={{1,4},{5,8},{9,12},{13,16},{17,20},{21,24},{25,28},{33,36},{37,40}... | collective-permute-start | bytes 122888 | tf_op jit(solution)/shard_map/ppermute | solution.py:86
  80.9 1.3 %collective-permute-start.21 = (bf16[2,20,512]{2,1,0:T(8,128)(2,1)S(1)}, bf16[2,20,512]{2,1,0:T(8,128)(2,1)S(1)}, u32[]{:S(2)}, u32[]{:S(2)}) collective-permute-start(bf16[2,20,512]{2,1,0:T(8,128)(2,1)S(1)} %collective-permute-done.20), channel_id=1, source_target_pairs={{2,4},{6,8},{10,12},{14,16},{18,20},{22,24},{26,28},{34,36},{38,40... | collective-permute-start | bytes 122888 | tf_op jit(solution)/shard_map/ppermute | solution.py:86
  82.2 5.0 %collective-permute-start.16 = (bf16[2,64,512]{2,1,0:T(8,128)(2,1)S(1)}, bf16[2,64,512]{2,1,0:T(8,128)(2,1)S(1)}, u32[]{:S(2)}, u32[]{:S(2)}) collective-permute-start(bf16[2,64,512]{2,1,0:T(8,128)(2,1)S(1)} %get-tuple-element.33), channel_id=1, source_target_pairs={{0,32},{1,33},{2,34},{3,35},{4,36},{5,37},{6,38},{7,39},{8,40},{9,... | collective-permute-start | bytes 393224 | tf_op jit(solution)/shard_map/ppermute | solution.py:62
  87.3 8.2 %collective-permute-done.17 = bf16[2,24,512]{2,1,0:T(8,128)(2,1)S(1)} collective-permute-done((bf16[2,24,512]{2,1,0:T(8,128)(2,1)S(1)}, bf16[2,24,512]{2,1,0:T(8,128)(2,1)S(1)}, u32[]{:S(2)}, u32[]{:S(2)}) %collective-permute-start.17) | collective-permute-done | bytes 49184 | tf_op jit(solution)/shard_map/ppermute | solution.py:86
  95.5 2.8 %collective-permute-done.21 = bf16[2,20,512]{2,1,0:T(8,128)(2,1)S(1)} collective-permute-done((bf16[2,20,512]{2,1,0:T(8,128)(2,1)S(1)}, bf16[2,20,512]{2,1,0:T(8,128)(2,1)S(1)}, u32[]{:S(2)}, u32[]{:S(2)}) %collective-permute-start.21) | collective-permute-done | bytes 40992 | tf_op jit(solution)/shard_map/ppermute | solution.py:86
  98.4 0.1 fusion.49
  98.5 1.5 %fusion = f32[2,64,2,1024]{3,1,2,0:T(8,128)S(1)} fusion(bf16[1,1,2,1024,1024]{4,3,2,1,0:T(8,128)(2,1)S(1)} %copy-done.1, bf16[1,64,1024]{2,1,0:T(8,128)(2,1)S(1)} %get-tuple-element.30, bf16[1,64,1024]{2,1,0:T(8,128)(2,1)S(1)} %get-tuple-element.29), kind=kOutput, calls=%fused_computation | convolution fusion | flops 537395200 | bytes 5505024 | tf_op jit(solution)/shard_map/dot_general | solution.py:39
  100.0 0.1 fusion.52
  100.2 1.1 %copy.9 = bf16[1,1,1024,2,128]{4,3,2,1,0:T(2,128)(2,1)} copy(bf16[1,1,1024,2,128]{2,4,3,1,0:T(8,128)(2,1)S(1)} %maximum_bitcast_fusion.8) | data formatting | bytes 1048576 | tf_op jit(solution)/shard_map/broadcast_in_dim | solution.py:116
  (45 shorter events, 0.5 us)
Async XLA Ops:
  4.3 10.5 %copy-start.6 = (f32[1,1,2,128]{3,2,1,0:T(2,128)S(1)}, f32[1,1,2,128]{3,2,1,0:T(2,128)}, u32[]{:S(2)}) copy-start(f32[1,1,2,128]{3,2,1,0:T(2,128)} %param.8) | copy-start | bytes 3076
  4.3 10.7 %copy-start.5 = (f32[3,2]{0,1:T(2,128)S(1)}, f32[3,2]{0,1:T(2,128)}, u32[]{:S(2)}) copy-start(f32[3,2]{0,1:T(2,128)} %param.9) | copy-start | bytes 76
  4.3 10.8 %copy-start.4 = (s32[1,1,1024]{2,1,0:T(1,128)S(1)}, s32[1,1,1024]{2,1,0:T(1,128)}, u32[]{:S(2)}) copy-start(s32[1,1,1024]{2,1,0:T(1,128)} %param.6) | copy-start | bytes 12292
  4.5 20.0 %collective-permute-start.1 = (bf16[2,48,512]{2,1,0:T(8,128)(2,1)S(1)}, bf16[2,48,512]{2,1,0:T(8,128)(2,1)S(1)}, u32[]{:S(2)}, u32[]{:S(2)}) collective-permute-start(bf16[2,48,512]{2,1,0:T(8,128)(2,1)S(1)} %fusion.55), channel_id=1, source_target_pairs={{3,4},{7,8},{11,12},{15,16},{19,20},{23,24},{27,28},{35,36},{39,40... | collective-permute-start | bytes 294920 | tf_op jit(solution)/shard_map/ppermute | solution.py:86
  5.8 11.3 %collective-permute-start.2 = (bf16[2,40,512]{2,1,0:T(8,128)(2,1)S(1)}, bf16[2,40,512]{2,1,0:T(8,128)(2,1)S(1)}, u32[]{:S(2)}, u32[]{:S(2)}) collective-permute-start(bf16[2,40,512]{2,1,0:T(8,128)(2,1)S(1)} %get-tuple-element.45), channel_id=1, source_target_pairs={{3,1},{7,5},{11,9},{15,13},{19,17},{23,21},{27,25},{35,33},{39,37}... | collective-permute-start | bytes 245768 | tf_op jit(solution)/shard_map/ppermute | solution.py:81
  6.5 12.2 %collective-permute-start.4 = (bf16[2,40,512]{2,1,0:T(8,128)(2,1)S(1)}, bf16[2,40,512]{2,1,0:T(8,128)(2,1)S(1)}, u32[]{:S(2)}, u32[]{:S(2)}) collective-permute-start(bf16[2,40,512]{2,1,0:T(8,128)(2,1)S(1)} %get-tuple-element.46), channel_id=1, source_target_pairs={{3,2},{7,6},{11,10},{15,14},{19,18},{23,22},{27,26},{35,34},{39,38... | collective-permute-start | bytes 245768 | tf_op jit(solution)/shard_map/ppermute | solution.py:81
  7.2 12.8 %collective-permute-start.6 = (bf16[2,128,512]{2,1,0:T(8,128)(2,1)S(1)}, bf16[2,128,512]{2,1,0:T(8,128)(2,1)S(1)}, u32[]{:S(2)}, u32[]{:S(2)}) collective-permute-start(bf16[2,128,512]{2,1,0:T(8,128)(2,1)S(1)} %get-tuple-element.43), channel_id=1, source_target_pairs={{0,1},{1,2},{2,3},{4,5},{5,6},{6,7},{8,9},{9,10},{10,11},{12,13},{... | collective-permute-start | bytes 786440 | tf_op jit(solution)/shard_map/ppermute | solution.py:66
  10.4 9.5 %collective-permute-start = (bf16[2,128,512]{2,1,0:T(8,128)(2,1)S(1)}, bf16[2,128,512]{2,1,0:T(8,128)(2,1)S(1)}, u32[]{:S(2)}, u32[]{:S(2)}) collective-permute-start(bf16[2,128,512]{2,1,0:T(8,128)(2,1)S(1)} %get-tuple-element.44), channel_id=1, source_target_pairs={{0,32},{1,33},{2,34},{3,35},{4,36},{5,37},{6,38},{7,39},{8,40},{9,... | collective-permute-start | bytes 786440 | tf_op jit(solution)/shard_map/ppermute | solution.py:62
  15.2 0.6 copy-start.2
  17.1 3.2 %copy-start = (bf16[1,1,2,1024,1024]{4,3,2,1,0:T(8,128)(2,1)S(1)}, bf16[1,1,2,1024,1024]{4,3,2,1,0:T(8,128)(2,1)}, u32[]{:S(2)}) copy-start(bf16[1,1,2,1024,1024]{4,3,2,1,0:T(8,128)(2,1)} %param.5) | copy-start | bytes 12582916
  17.1 17.5 %collective-permute-start.3 = (bf16[2,40,512]{2,1,0:T(8,128)(2,1)S(1)}, bf16[2,40,512]{2,1,0:T(8,128)(2,1)S(1)}, u32[]{:S(2)}, u32[]{:S(2)}) collective-permute-start(bf16[2,40,512]{2,1,0:T(8,128)(2,1)S(1)} %collective-permute-done.2), channel_id=1, source_target_pairs={{1,4},{5,8},{9,12},{13,16},{17,20},{21,24},{25,28},{33,36},{37,40}... | collective-permute-start | bytes 245768 | tf_op jit(solution)/shard_map/ppermute | solution.py:86
  18.7 20.4 %collective-permute-start.5 = (bf16[2,40,512]{2,1,0:T(8,128)(2,1)S(1)}, bf16[2,40,512]{2,1,0:T(8,128)(2,1)S(1)}, u32[]{:S(2)}, u32[]{:S(2)}) collective-permute-start(bf16[2,40,512]{2,1,0:T(8,128)(2,1)S(1)} %collective-permute-done.4), channel_id=1, source_target_pairs={{2,4},{6,8},{10,12},{14,16},{18,20},{22,24},{26,28},{34,36},{38,40... | collective-permute-start | bytes 245768 | tf_op jit(solution)/shard_map/ppermute | solution.py:86
  20.4 2.9 %copy-start.3 = (f32[2,1024]{1,0:T(2,128)S(1)}, f32[2,1024]{1,0:T(2,128)}, u32[]{:S(2)}) copy-start(f32[2,1024]{1,0:T(2,128)} %shard_map.55) | copy-start | bytes 24580
  21.9 17.2 %collective-permute-start.7 = (bf16[2,128,512]{2,1,0:T(8,128)(2,1)S(1)}, bf16[2,128,512]{2,1,0:T(8,128)(2,1)S(1)}, u32[]{:S(2)}, u32[]{:S(2)}) collective-permute-start(bf16[2,128,512]{2,1,0:T(8,128)(2,1)S(1)} %get-tuple-element.41), channel_id=1, source_target_pairs={{1,33},{2,34},{3,35},{5,37},{6,38},{7,39},{9,41},{10,42},{11,43},{... | collective-permute-start | bytes 786440 | tf_op jit(solution)/shard_map/ppermute | solution.py:62
  22.6 16.5 %collective-permute-start.8 = (bf16[2,128,512]{2,1,0:T(8,128)(2,1)S(1)}, bf16[2,128,512]{2,1,0:T(8,128)(2,1)S(1)}, u32[]{:S(2)}, u32[]{:S(2)}) collective-permute-start(bf16[2,128,512]{2,1,0:T(8,128)(2,1)S(1)} %get-tuple-element.42), channel_id=1, source_target_pairs={{1,2},{2,3},{5,6},{6,7},{9,10},{10,11},{13,14},{14,15},{17,18},{18... | collective-permute-start | bytes 786440 | tf_op jit(solution)/shard_map/ppermute | solution.py:66
  23.3 16.2 %copy-start.1 = (bf16[1,1,2,1024,1024]{4,3,2,1,0:T(8,128)(2,1)S(1)}, bf16[1,1,2,1024,1024]{4,3,2,1,0:T(8,128)(2,1)}, u32[]{:S(2)}) copy-start(bf16[1,1,2,1024,1024]{4,3,2,1,0:T(8,128)(2,1)} %param.5) | copy-start | bytes 12582916
  42.8 26.0 %collective-permute-start.9 = (bf16[2,128,512]{2,1,0:T(8,128)(2,1)S(1)}, bf16[2,128,512]{2,1,0:T(8,128)(2,1)S(1)}, u32[]{:S(2)}, u32[]{:S(2)}) collective-permute-start(bf16[2,128,512]{2,1,0:T(8,128)(2,1)S(1)} %get-tuple-element.37), channel_id=1, source_target_pairs={{0,32},{4,36},{8,40},{12,44},{16,48},{20,52},{24,56},{28,60},{32,6... | collective-permute-start | bytes 786440 | tf_op jit(solution)/shard_map/ppermute | solution.py:62
  46.9 2.7 %collective-permute-start.11 = (bf16[2,40,512]{2,1,0:T(8,128)(2,1)S(1)}, bf16[2,40,512]{2,1,0:T(8,128)(2,1)S(1)}, u32[]{:S(2)}, u32[]{:S(2)}) collective-permute-start(bf16[2,40,512]{2,1,0:T(8,128)(2,1)S(1)} %get-tuple-element.39), channel_id=1, source_target_pairs={{3,1},{7,5},{11,9},{15,13},{19,17},{23,21},{27,25},{35,33},{39,37}... | collective-permute-start | bytes 245768 | tf_op jit(solution)/shard_map/ppermute | solution.py:81
  47.6 3.3 %collective-permute-start.13 = (bf16[2,40,512]{2,1,0:T(8,128)(2,1)S(1)}, bf16[2,40,512]{2,1,0:T(8,128)(2,1)S(1)}, u32[]{:S(2)}, u32[]{:S(2)}) collective-permute-start(bf16[2,40,512]{2,1,0:T(8,128)(2,1)S(1)} %get-tuple-element.40), channel_id=1, source_target_pairs={{3,2},{7,6},{11,10},{15,14},{19,18},{23,22},{27,26},{35,34},{39,38... | collective-permute-start | bytes 245768 | tf_op jit(solution)/shard_map/ppermute | solution.py:81
  48.3 21.2 %collective-permute-start.10 = (bf16[2,48,512]{2,1,0:T(8,128)(2,1)S(1)}, bf16[2,48,512]{2,1,0:T(8,128)(2,1)S(1)}, u32[]{:S(2)}, u32[]{:S(2)}) collective-permute-start(bf16[2,48,512]{2,1,0:T(8,128)(2,1)S(1)} %fusion.54), channel_id=1, source_target_pairs={{3,4},{7,8},{11,12},{15,16},{19,20},{23,24},{27,28},{35,36},{39,40... | collective-permute-start | bytes 294920 | tf_op jit(solution)/shard_map/ppermute | solution.py:86
  49.6 20.6 %collective-permute-start.12 = (bf16[2,40,512]{2,1,0:T(8,128)(2,1)S(1)}, bf16[2,40,512]{2,1,0:T(8,128)(2,1)S(1)}, u32[]{:S(2)}, u32[]{:S(2)}) collective-permute-start(bf16[2,40,512]{2,1,0:T(8,128)(2,1)S(1)} %collective-permute-done.11), channel_id=1, source_target_pairs={{1,4},{5,8},{9,12},{13,16},{17,20},{21,24},{25,28},{33,36},{37,40}... | collective-permute-start | bytes 245768 | tf_op jit(solution)/shard_map/ppermute | solution.py:86
  50.9 19.3 %collective-permute-start.14 = (bf16[2,40,512]{2,1,0:T(8,128)(2,1)S(1)}, bf16[2,40,512]{2,1,0:T(8,128)(2,1)S(1)}, u32[]{:S(2)}, u32[]{:S(2)}) collective-permute-start(bf16[2,40,512]{2,1,0:T(8,128)(2,1)S(1)} %collective-permute-done.13), channel_id=1, source_target_pairs={{2,4},{6,8},{10,12},{14,16},{18,20},{22,24},{26,28},{34,36},{38,40... | collective-permute-start | bytes 245768 | tf_op jit(solution)/shard_map/ppermute | solution.py:86
  52.2 20.3 %collective-permute-start.15 = (bf16[2,128,512]{2,1,0:T(8,128)(2,1)S(1)}, bf16[2,128,512]{2,1,0:T(8,128)(2,1)S(1)}, u32[]{:S(2)}, u32[]{:S(2)}) collective-permute-start(bf16[2,128,512]{2,1,0:T(8,128)(2,1)S(1)} %get-tuple-element.38), channel_id=1, source_target_pairs={{0,1},{4,5},{8,9},{12,13},{16,17},{20,21},{24,25},{28,29},{32,33},... | collective-permute-start | bytes 786440 | tf_op jit(solution)/shard_map/ppermute | solution.py:66
  68.8 10.8 %collective-permute-start.18 = (bf16[2,20,512]{2,1,0:T(8,128)(2,1)S(1)}, bf16[2,20,512]{2,1,0:T(8,128)(2,1)S(1)}, u32[]{:S(2)}, u32[]{:S(2)}) collective-permute-start(bf16[2,20,512]{2,1,0:T(8,128)(2,1)S(1)} %get-tuple-element.35), channel_id=1, source_target_pairs={{3,1},{7,5},{11,9},{15,13},{19,17},{23,21},{27,25},{35,33},{39,37}... | collective-permute-start | bytes 122888 | tf_op jit(solution)/shard_map/ppermute | solution.py:81
  69.5 11.4 %collective-permute-start.20 = (bf16[2,20,512]{2,1,0:T(8,128)(2,1)S(1)}, bf16[2,20,512]{2,1,0:T(8,128)(2,1)S(1)}, u32[]{:S(2)}, u32[]{:S(2)}) collective-permute-start(bf16[2,20,512]{2,1,0:T(8,128)(2,1)S(1)} %get-tuple-element.36), channel_id=1, source_target_pairs={{3,2},{7,6},{11,10},{15,14},{19,18},{23,22},{27,26},{35,34},{39,38... | collective-permute-start | bytes 122888 | tf_op jit(solution)/shard_map/ppermute | solution.py:81
  74.5 23.8 %collective-permute-start.22 = (bf16[2,64,512]{2,1,0:T(8,128)(2,1)S(1)}, bf16[2,64,512]{2,1,0:T(8,128)(2,1)S(1)}, u32[]{:S(2)}, u32[]{:S(2)}) collective-permute-start(bf16[2,64,512]{2,1,0:T(8,128)(2,1)S(1)} %get-tuple-element.34), channel_id=1, source_target_pairs={{0,1},{1,2},{2,3},{4,5},{5,6},{6,7},{8,9},{9,10},{10,11},{12,13},{... | collective-permute-start | bytes 393224 | tf_op jit(solution)/shard_map/ppermute | solution.py:66
  78.3 17.2 %collective-permute-start.17 = (bf16[2,24,512]{2,1,0:T(8,128)(2,1)S(1)}, bf16[2,24,512]{2,1,0:T(8,128)(2,1)S(1)}, u32[]{:S(2)}, u32[]{:S(2)}) collective-permute-start(bf16[2,24,512]{2,1,0:T(8,128)(2,1)S(1)} %fusion.59), channel_id=1, source_target_pairs={{3,4},{7,8},{11,12},{15,16},{19,20},{23,24},{27,28},{35,36},{39,40... | collective-permute-start | bytes 147464 | tf_op jit(solution)/shard_map/ppermute | solution.py:86
  79.6 15.9 %collective-permute-start.19 = (bf16[2,20,512]{2,1,0:T(8,128)(2,1)S(1)}, bf16[2,20,512]{2,1,0:T(8,128)(2,1)S(1)}, u32[]{:S(2)}, u32[]{:S(2)}) collective-permute-start(bf16[2,20,512]{2,1,0:T(8,128)(2,1)S(1)} %collective-permute-done.18), channel_id=1, source_target_pairs={{1,4},{5,8},{9,12},{13,16},{17,20},{21,24},{25,28},{33,36},{37,40}... | collective-permute-start | bytes 122888 | tf_op jit(solution)/shard_map/ppermute | solution.py:86
  80.9 17.4 %collective-permute-start.21 = (bf16[2,20,512]{2,1,0:T(8,128)(2,1)S(1)}, bf16[2,20,512]{2,1,0:T(8,128)(2,1)S(1)}, u32[]{:S(2)}, u32[]{:S(2)}) collective-permute-start(bf16[2,20,512]{2,1,0:T(8,128)(2,1)S(1)} %collective-permute-done.20), channel_id=1, source_target_pairs={{2,4},{6,8},{10,12},{14,16},{18,20},{22,24},{26,28},{34,36},{38,40... | collective-permute-start | bytes 122888 | tf_op jit(solution)/shard_map/ppermute | solution.py:86
  82.2 16.1 %collective-permute-start.16 = (bf16[2,64,512]{2,1,0:T(8,128)(2,1)S(1)}, bf16[2,64,512]{2,1,0:T(8,128)(2,1)S(1)}, u32[]{:S(2)}, u32[]{:S(2)}) collective-permute-start(bf16[2,64,512]{2,1,0:T(8,128)(2,1)S(1)} %get-tuple-element.33), channel_id=1, source_target_pairs={{0,32},{1,33},{2,34},{3,35},{4,36},{5,37},{6,38},{7,39},{8,40},{9,... | collective-permute-start | bytes 393224 | tf_op jit(solution)/shard_map/ppermute | solution.py:62

commit v3 on v2

--- a/solution.py
+++ b/solution.py
@@ -7,7 +7,7 @@
 
 NB = 64
 BLOCK = 4
-PIECES = ((3, 48), (1, 40), (2, 40))
+PIECES = {1: ((3, 64), (2, 64)), 2: ((3, 64), (2, 64)), 3: ((3, 32), (2, 32))}
 
 
 def copy_kernel(source_ref, target_ref):
@@ -65,13 +65,11 @@
         pairs = [(j, j + 1) for j in range(n_gy) if j % BLOCK in lanes]
         return lax.ppermute(traces[:, :, face:], "gy", pairs)
 
-    def cross(traces):
+    def cross(traces, name):
         north = traces[:, :, face:]
-        live = north.shape[1]
         at = 0
         pieces = []
-        for column, share in PIECES:
-            size = share * live // width
+        for column, size in PIECES[int(name[1])]:
             pieces.append((column, north[:, at : at + size]))
             at += size
         moved = []
@@ -89,17 +87,19 @@
     t0 = apply(source.astype(jnp.bfloat16))
     w1 = east_to(t0, (0, 1, 2, 3))
     s1 = north_to(t0, (0, 1, 2))
-    x1 = cross(t0)
+    x1 = cross(t0, "x1")
 
     t1 = step(w1, s1)
     w2 = east_to(t1, (1, 2, 3))
     s2 = north_to(t1, (1, 2))
-    x2 = cross(t1)
+    x2 = cross(t1, "x2")
 
     t2 = step(w2, s2)
-    x3 = cross(t2[:, :NB])
+    x3 = cross(t2[:, :NB], "x3")
 
-    factor = pl.pallas_call(copy_kernel, out_shape=jax.ShapeDtypeStruct(factor.shape, factor.dtype))(factor)
+    factor = pl.pallas_call(
+        copy_kernel, out_shape=jax.ShapeDtypeStruct(factor.shape, factor.dtype)
+    )(factor)
     w1, x1, t2 = lax.optimization_barrier((w1, x1, t2))
     late1 = step(w1, x1)
     w3 = east_to(late1, (0,))

time: 103 us -> 105 us (1.019)
  the two profiles are of different devices: /device:TPU:7 before, /device:TPU:166 now
where the time goes in v3:
time: 105 us
  waiting for transfers between devices  58.3 us (56%)
  starting transfers between devices  28.1 us (27%)
  matrix products  10.2 us (10%)
  other arithmetic  4.38 us (4%)
  local copies, waits for them, and re-layouts  2.15 us (2%)
  Pallas kernels  1.29 us (1%)
    ppermute x6, waiting for transfers between devices, cross(): arrived.append(lax.ppermute(piece, 'gy', pairs))  57.1 us
    ppermute x4, starting transfers between devices, east_to(): return lax.ppermute(traces[:, :, :face], ('gx', 'gy'), pairs)  11.8 us
    dot_general x6, matrix products, apply(): lax.dot_general(flat, operator, (((1,), (2,)), ((), ())), preferred_eleme...  10.2 us
    ppermute x6, starting transfers between devices, cross(): arrived.append(lax.ppermute(piece, 'gy', pairs))  8.15 us
    ppermute x4, starting transfers between devices, north_to(): return lax.ppermute(traces[:, :, face:], 'gy', pairs)  6.15 us
  transfers between devices with their start and end apart: 17, of which 7 were waited for; matrix products, arithmetic and copies ran while one was open for 5% of the time, Pallas kernels for 1%

profile of v3, /device:TPU:166, one launch (start us, length us, event | category | flops | bytes accessed | tf_op | source)
XLA Modules:
  0.0 105.0 jit_solution(16885750334243235539)
XLA Ops:
  0.0 0.8 iota_compare_fusion
  0.8 0.0 copy-start.5
  0.8 3.5 %fusion.10 = f32[2,128,2,1024]{3,1,2,0:T(8,128)S(1)} fusion(bf16[1,1,2,1024,1024]{4,3,2,1,0:T(8,128)(2,1)} %param.5, f32[2,128]{1,0:T(2,128)} %bitcast.91, pred[128,1024]{1,0:T(8,128)(4,1)S(1)} %iota_compare_fusion), kind=kOutput, calls=%fused_computation.10 | convolution fusion | flops 1074003968 | bytes 6423552 | tf_op jit(solution)/shard_map/dot_general | solution.py:39
  4.3 0.0 copy-start.4
  4.3 0.0 copy-start.3
  4.3 0.1 fusion.34
  4.5 1.3 %collective-permute-start.1 = (bf16[2,64,512]{2,1,0:T(8,128)(2,1)S(1)}, bf16[2,64,512]{2,1,0:T(8,128)(2,1)S(1)}, u32[]{:S(2)}, u32[]{:S(2)}) collective-permute-start(bf16[2,64,512]{2,1,0:T(8,128)(2,1)S(1)} %get-tuple-element.45), channel_id=1, source_target_pairs={{3,4},{7,8},{11,12},{15,16},{19,20},{23,24},{27,28},{35,36},{39,40... | collective-permute-start | bytes 393224 | tf_op jit(solution)/shard_map/ppermute | solution.py:84
  5.8 0.7 collective-permute-start.2
  6.5 2.9 %collective-permute-start.4 = (bf16[2,128,512]{2,1,0:T(8,128)(2,1)S(1)}, bf16[2,128,512]{2,1,0:T(8,128)(2,1)S(1)}, u32[]{:S(2)}, u32[]{:S(2)}) collective-permute-start(bf16[2,128,512]{2,1,0:T(8,128)(2,1)S(1)} %get-tuple-element.43), channel_id=1, source_target_pairs={{0,1},{1,2},{2,3},{4,5},{5,6},{6,7},{8,9},{9,10},{10,11},{12,13},{... | collective-permute-start | bytes 786440 | tf_op jit(solution)/shard_map/ppermute | solution.py:66
  9.4 1.9 %collective-permute-start = (bf16[2,128,512]{2,1,0:T(8,128)(2,1)S(1)}, bf16[2,128,512]{2,1,0:T(8,128)(2,1)S(1)}, u32[]{:S(2)}, u32[]{:S(2)}) collective-permute-start(bf16[2,128,512]{2,1,0:T(8,128)(2,1)S(1)} %get-tuple-element.44), channel_id=1, source_target_pairs={{0,32},{1,33},{2,34},{3,35},{4,36},{5,37},{6,38},{7,39},{8,40},{9,... | collective-permute-start | bytes 786440 | tf_op jit(solution)/shard_map/ppermute | solution.py:62
  11.4 0.2 broadcast_select_fusion
  11.5 0.1 copy.8
  11.6 0.7 select_reduce_fusion.source_ref
  12.3 1.3 %shard_map.55 = f32[2,1024]{1,0:T(2,128)} custom-call(f32[2,1024]{1,0:T(2,128)} %select_reduce_fusion.source_ref), custom_call_target="tpu_custom_call" | custom-call | tf_op jit(solution)/shard_map/pallas_call | solution.py:100
  13.6 0.9 fusion.67
  14.5 0.0 collective-permute-done.2
  14.5 1.4 %collective-permute-start.3 = (bf16[2,64,512]{2,1,0:T(8,128)(2,1)S(1)}, bf16[2,64,512]{2,1,0:T(8,128)(2,1)S(1)}, u32[]{:S(2)}, u32[]{:S(2)}) collective-permute-start(bf16[2,64,512]{2,1,0:T(8,128)(2,1)S(1)} %collective-permute-done.2), channel_id=1, source_target_pairs={{2,4},{6,8},{10,12},{14,16},{18,20},{22,24},{26,28},{34,36},{38,40... | collective-permute-start | bytes 393224 | tf_op jit(solution)/shard_map/ppermute | solution.py:84
  15.9 0.0 collective-permute-done.4
  15.9 1.2 %collective-permute-done = bf16[2,128,512]{2,1,0:T(8,128)(2,1)S(1)} collective-permute-done((bf16[2,128,512]{2,1,0:T(8,128)(2,1)S(1)}, bf16[2,128,512]{2,1,0:T(8,128)(2,1)S(1)}, u32[]{:S(2)}, u32[]{:S(2)}) %collective-permute-start) | collective-permute-done | bytes 262176 | tf_op jit(solution)/shard_map/ppermute | solution.py:62
  17.1 0.1 maximum_convert_fusion
  17.2 0.2 add_convert_fusion.7
  17.5 1.3 %fusion.8 = f32[2,128,2,1024]{3,1,2,0:T(8,128)S(1)} fusion(bf16[1,1,2,1024,1024]{4,3,2,1,0:T(8,128)(2,1)S(1)} %copy-done, bf16[1,128,1024]{2,1,0:T(8,128)(2,1)S(1)} %get-tuple-element.18, bf16[1,128,1024]{2,1,0:T(8,128)(2,1)S(1)} %get-tuple-element.17), kind=kOutput, calls=%fused_computation.8 | convolution fusion | flops 1074790400 | bytes 6815744 | tf_op jit(solution)/shard_map/dot_general | solution.py:39
  18.8 0.1 fusion.36
  19.0 0.7 collective-permute-start.5
  19.7 0.7 collective-permute-start.6
  20.4 3.2 %collective-permute-done.1 = bf16[2,64,512]{2,1,0:T(8,128)(2,1)S(1)} collective-permute-done((bf16[2,64,512]{2,1,0:T(8,128)(2,1)S(1)}, bf16[2,64,512]{2,1,0:T(8,128)(2,1)S(1)}, u32[]{:S(2)}, u32[]{:S(2)}) %collective-permute-start.1) | collective-permute-done | bytes 131104 | tf_op jit(solution)/shard_map/ppermute | solution.py:84
  23.6 14.5 %collective-permute-done.3 = bf16[2,64,512]{2,1,0:T(8,128)(2,1)S(1)} collective-permute-done((bf16[2,64,512]{2,1,0:T(8,128)(2,1)S(1)}, bf16[2,64,512]{2,1,0:T(8,128)(2,1)S(1)}, u32[]{:S(2)}, u32[]{:S(2)}) %collective-permute-start.3) | collective-permute-done | bytes 131104 | tf_op jit(solution)/shard_map/ppermute | solution.py:84
  38.1 0.0 collective-permute-done.5
  38.1 0.0 collective-permute-done.6
  38.1 0.1 maximum_convert_fusion.1
  38.2 0.2 add_convert_fusion.5
  38.5 1.3 %fusion.6 = f32[2,128,2,1024]{3,1,2,0:T(8,128)S(1)} fusion(bf16[1,1,2,1024,1024]{4,3,2,1,0:T(8,128)(2,1)S(1)} %copy-done, bf16[1,128,1024]{2,1,0:T(8,128)(2,1)S(1)} %get-tuple-element.16, bf16[1,128,1024]{2,1,0:T(8,128)(2,1)S(1)} %get-tuple-element.15), kind=kOutput, calls=%fused_computation.6 | convolution fusion | flops 1074790400 | bytes 6815744 | tf_op jit(solution)/shard_map/dot_general | solution.py:39
  39.8 0.1 fusion.37
  39.9 0.1 pad_maximum_fusion
  40.0 0.1 maximum_convert_fusion.2
  40.1 0.2 add_convert_fusion.3
  40.3 1.3 %fusion.4 = f32[2,128,2,1024]{3,1,2,0:T(8,128)S(1)} fusion(bf16[1,1,2,1024,1024]{4,3,2,1,0:T(8,128)(2,1)S(1)} %copy-done, bf16[1,128,1024]{2,1,0:T(8,128)(2,1)S(1)} %get-tuple-element.14, bf16[1,128,1024]{2,1,0:T(8,128)(2,1)S(1)} %get-tuple-element.13), kind=kOutput, calls=%fused_computation.4 | convolution fusion | flops 1074790400 | bytes 6815744 | tf_op jit(solution)/shard_map/dot_general | solution.py:39
  41.6 0.1 fusion.39
  41.8 7.1 %collective-permute-start.7 = (bf16[2,128,512]{2,1,0:T(8,128)(2,1)S(1)}, bf16[2,128,512]{2,1,0:T(8,128)(2,1)S(1)}, u32[]{:S(2)}, u32[]{:S(2)}) collective-permute-start(bf16[2,128,512]{2,1,0:T(8,128)(2,1)S(1)} %get-tuple-element.37), channel_id=1, source_target_pairs={{0,32},{4,36},{8,40},{12,44},{16,48},{20,52},{24,56},{28,60},{32,6... | collective-permute-start | bytes 786440 | tf_op jit(solution)/shard_map/ppermute | solution.py:62
  49.0 0.7 collective-permute-start.9
  49.7 0.0 copy-start.1
  49.7 1.6 %collective-permute-start.8 = (bf16[2,64,512]{2,1,0:T(8,128)(2,1)S(1)}, bf16[2,64,512]{2,1,0:T(8,128)(2,1)S(1)}, u32[]{:S(2)}, u32[]{:S(2)}) collective-permute-start(bf16[2,64,512]{2,1,0:T(8,128)(2,1)S(1)} %get-tuple-element.39), channel_id=1, source_target_pairs={{3,4},{7,8},{11,12},{15,16},{19,20},{23,24},{27,28},{35,36},{39,40... | collective-permute-start | bytes 393224 | tf_op jit(solution)/shard_map/ppermute | solution.py:84
  51.2 1.3 %collective-permute-start.10 = (bf16[2,64,512]{2,1,0:T(8,128)(2,1)S(1)}, bf16[2,64,512]{2,1,0:T(8,128)(2,1)S(1)}, u32[]{:S(2)}, u32[]{:S(2)}) collective-permute-start(bf16[2,64,512]{2,1,0:T(8,128)(2,1)S(1)} %collective-permute-done.9), channel_id=1, source_target_pairs={{2,4},{6,8},{10,12},{14,16},{18,20},{22,24},{26,28},{34,36},{38,40... | collective-permute-start | bytes 393224 | tf_op jit(solution)/shard_map/ppermute | solution.py:84
  52.5 1.3 %collective-permute-start.11 = (bf16[2,128,512]{2,1,0:T(8,128)(2,1)S(1)}, bf16[2,128,512]{2,1,0:T(8,128)(2,1)S(1)}, u32[]{:S(2)}, u32[]{:S(2)}) collective-permute-start(bf16[2,128,512]{2,1,0:T(8,128)(2,1)S(1)} %get-tuple-element.38), channel_id=1, source_target_pairs={{0,1},{4,5},{8,9},{12,13},{16,17},{20,21},{24,25},{28,29},{32,33},... | collective-permute-start | bytes 786440 | tf_op jit(solution)/shard_map/ppermute | solution.py:66
  53.9 0.7 collective-permute-start.14
  54.6 0.0 collective-permute-done.7
  54.6 15.1 %collective-permute-done.8 = bf16[2,64,512]{2,1,0:T(8,128)(2,1)S(1)} collective-permute-done((bf16[2,64,512]{2,1,0:T(8,128)(2,1)S(1)}, bf16[2,64,512]{2,1,0:T(8,128)(2,1)S(1)}, u32[]{:S(2)}, u32[]{:S(2)}) %collective-permute-start.8) | collective-permute-done | bytes 131104 | tf_op jit(solution)/shard_map/ppermute | solution.py:84
  69.7 8.5 %collective-permute-done.10 = bf16[2,64,512]{2,1,0:T(8,128)(2,1)S(1)} collective-permute-done((bf16[2,64,512]{2,1,0:T(8,128)(2,1)S(1)}, bf16[2,64,512]{2,1,0:T(8,128)(2,1)S(1)}, u32[]{:S(2)}, u32[]{:S(2)}) %collective-permute-start.10) | collective-permute-done | bytes 131104 | tf_op jit(solution)/shard_map/ppermute | solution.py:84
  78.2 0.1 maximum_select_fusion.1
  78.3 0.1 maximum_convert_fusion.3
  78.4 0.2 add_convert_fusion.1
  78.7 1.3 %fusion.2 = f32[2,128,2,1024]{3,1,2,0:T(8,128)S(1)} fusion(bf16[1,1,2,1024,1024]{4,3,2,1,0:T(8,128)(2,1)S(1)} %copy-done.1, bf16[1,128,1024]{2,1,0:T(8,128)(2,1)S(1)} %get-tuple-element.12, bf16[1,128,1024]{2,1,0:T(8,128)(2,1)S(1)} %get-tuple-element.11), kind=kOutput, calls=%fused_computation.2 | convolution fusion | flops 1074790400 | bytes 6815744 | tf_op jit(solution)/shard_map/dot_general | solution.py:39
  80.0 0.1 fusion.41
  80.1 0.1 maximum_select_fusion
  80.2 1.3 %collective-permute-start.16 = (bf16[2,64,512]{2,1,0:T(8,128)(2,1)S(1)}, bf16[2,64,512]{2,1,0:T(8,128)(2,1)S(1)}, u32[]{:S(2)}, u32[]{:S(2)}) collective-permute-start(bf16[2,64,512]{2,1,0:T(8,128)(2,1)S(1)} %get-tuple-element.34), channel_id=1, source_target_pairs={{0,1},{1,2},{2,3},{4,5},{5,6},{6,7},{8,9},{9,10},{10,11},{12,13},{... | collective-permute-start | bytes 393224 | tf_op jit(solution)/shard_map/ppermute | solution.py:66
  81.5 1.3 %collective-permute-start.13 = (bf16[2,32,512]{2,1,0:T(8,128)(2,1)S(1)}, bf16[2,32,512]{2,1,0:T(8,128)(2,1)S(1)}, u32[]{:S(2)}, u32[]{:S(2)}) collective-permute-start(bf16[2,32,512]{2,1,0:T(8,128)(2,1)S(1)} %get-tuple-element.35), channel_id=1, source_target_pairs={{3,4},{7,8},{11,12},{15,16},{19,20},{23,24},{27,28},{35,36},{39,40... | collective-permute-start | bytes 196616 | tf_op jit(solution)/shard_map/ppermute | solution.py:84
  82.8 1.3 %collective-permute-start.15 = (bf16[2,32,512]{2,1,0:T(8,128)(2,1)S(1)}, bf16[2,32,512]{2,1,0:T(8,128)(2,1)S(1)}, u32[]{:S(2)}, u32[]{:S(2)}) collective-permute-start(bf16[2,32,512]{2,1,0:T(8,128)(2,1)S(1)} %collective-permute-done.14), channel_id=1, source_target_pairs={{2,4},{6,8},{10,12},{14,16},{18,20},{22,24},{26,28},{34,36},{38,40... | collective-permute-start | bytes 196616 | tf_op jit(solution)/shard_map/ppermute | solution.py:84
  84.2 2.0 %collective-permute-start.12 = (bf16[2,64,512]{2,1,0:T(8,128)(2,1)S(1)}, bf16[2,64,512]{2,1,0:T(8,128)(2,1)S(1)}, u32[]{:S(2)}, u32[]{:S(2)}) collective-permute-start(bf16[2,64,512]{2,1,0:T(8,128)(2,1)S(1)} %get-tuple-element.33), channel_id=1, source_target_pairs={{0,32},{1,33},{2,34},{3,35},{4,36},{5,37},{6,38},{7,39},{8,40},{9,... | collective-permute-start | bytes 393224 | tf_op jit(solution)/shard_map/ppermute | solution.py:62
  86.2 14.6 %collective-permute-done.13 = bf16[2,32,512]{2,1,0:T(8,128)(2,1)S(1)} collective-permute-done((bf16[2,32,512]{2,1,0:T(8,128)(2,1)S(1)}, bf16[2,32,512]{2,1,0:T(8,128)(2,1)S(1)}, u32[]{:S(2)}, u32[]{:S(2)}) %collective-permute-start.13) | collective-permute-done | bytes 65568 | tf_op jit(solution)/shard_map/ppermute | solution.py:84
  100.8 1.2 %collective-permute-done.15 = bf16[2,32,512]{2,1,0:T(8,128)(2,1)S(1)} collective-permute-done((bf16[2,32,512]{2,1,0:T(8,128)(2,1)S(1)}, bf16[2,32,512]{2,1,0:T(8,128)(2,1)S(1)}, u32[]{:S(2)}, u32[]{:S(2)}) %collective-permute-start.15) | collective-permute-done | bytes 65568 | tf_op jit(solution)/shard_map/ppermute | solution.py:84
  102.1 0.1 fusion.49
  102.2 1.5 %fusion = f32[2,64,2,1024]{3,1,2,0:T(8,128)S(1)} fusion(bf16[1,1,2,1024,1024]{4,3,2,1,0:T(8,128)(2,1)S(1)} %copy-done.1, bf16[1,64,1024]{2,1,0:T(8,128)(2,1)S(1)} %get-tuple-element.30, bf16[1,64,1024]{2,1,0:T(8,128)(2,1)S(1)} %get-tuple-element.29), kind=kOutput, calls=%fused_computation | convolution fusion | flops 537395200 | bytes 5505024 | tf_op jit(solution)/shard_map/dot_general | solution.py:39
  103.8 0.1 fusion.52
  103.9 1.1 %copy.9 = bf16[1,1,1024,2,128]{4,3,2,1,0:T(2,128)(2,1)} copy(bf16[1,1,1024,2,128]{2,4,3,1,0:T(8,128)(2,1)S(1)} %maximum_bitcast_fusion.8) | data formatting | bytes 1048576 | tf_op jit(solution)/shard_map/broadcast_in_dim | solution.py:116
  (28 shorter events, 0.4 us)
Async XLA Ops:
  0.8 10.5 %copy-start.5 = (f32[1,1,2,128]{3,2,1,0:T(2,128)S(1)}, f32[1,1,2,128]{3,2,1,0:T(2,128)}, u32[]{:S(2)}) copy-start(f32[1,1,2,128]{3,2,1,0:T(2,128)} %param.8) | copy-start | bytes 3076
  4.3 7.2 %copy-start.4 = (f32[3,2]{0,1:T(2,128)S(1)}, f32[3,2]{0,1:T(2,128)}, u32[]{:S(2)}) copy-start(f32[3,2]{0,1:T(2,128)} %param.9) | copy-start | bytes 76
  4.3 7.3 %copy-start.3 = (s32[1,1,1024]{2,1,0:T(1,128)S(1)}, s32[1,1,1024]{2,1,0:T(1,128)}, u32[]{:S(2)}) copy-start(s32[1,1,1024]{2,1,0:T(1,128)} %param.6) | copy-start | bytes 12292
  4.5 19.1 %collective-permute-start.1 = (bf16[2,64,512]{2,1,0:T(8,128)(2,1)S(1)}, bf16[2,64,512]{2,1,0:T(8,128)(2,1)S(1)}, u32[]{:S(2)}, u32[]{:S(2)}) collective-permute-start(bf16[2,64,512]{2,1,0:T(8,128)(2,1)S(1)} %get-tuple-element.45), channel_id=1, source_target_pairs={{3,4},{7,8},{11,12},{15,16},{19,20},{23,24},{27,28},{35,36},{39,40... | collective-permute-start | bytes 393224 | tf_op jit(solution)/shard_map/ppermute | solution.py:84
  5.8 8.7 %collective-permute-start.2 = (bf16[2,64,512]{2,1,0:T(8,128)(2,1)S(1)}, bf16[2,64,512]{2,1,0:T(8,128)(2,1)S(1)}, u32[]{:S(2)}, u32[]{:S(2)}) collective-permute-start(bf16[2,64,512]{2,1,0:T(8,128)(2,1)S(1)} %get-tuple-element.46), channel_id=1, source_target_pairs={{3,2},{7,6},{11,10},{15,14},{19,18},{23,22},{27,26},{35,34},{39,38... | collective-permute-start | bytes 393224 | tf_op jit(solution)/shard_map/ppermute | solution.py:79
  6.5 9.4 %collective-permute-start.4 = (bf16[2,128,512]{2,1,0:T(8,128)(2,1)S(1)}, bf16[2,128,512]{2,1,0:T(8,128)(2,1)S(1)}, u32[]{:S(2)}, u32[]{:S(2)}) collective-permute-start(bf16[2,128,512]{2,1,0:T(8,128)(2,1)S(1)} %get-tuple-element.43), channel_id=1, source_target_pairs={{0,1},{1,2},{2,3},{4,5},{5,6},{6,7},{8,9},{9,10},{10,11},{12,13},{... | collective-permute-start | bytes 786440 | tf_op jit(solution)/shard_map/ppermute | solution.py:66
  9.4 7.7 %collective-permute-start = (bf16[2,128,512]{2,1,0:T(8,128)(2,1)S(1)}, bf16[2,128,512]{2,1,0:T(8,128)(2,1)S(1)}, u32[]{:S(2)}, u32[]{:S(2)}) collective-permute-start(bf16[2,128,512]{2,1,0:T(8,128)(2,1)S(1)} %get-tuple-element.44), channel_id=1, source_target_pairs={{0,32},{1,33},{2,34},{3,35},{4,36},{5,37},{6,38},{7,39},{8,40},{9,... | collective-permute-start | bytes 786440 | tf_op jit(solution)/shard_map/ppermute | solution.py:62
  13.6 3.9 %copy-start = (bf16[1,1,2,1024,1024]{4,3,2,1,0:T(8,128)(2,1)S(1)}, bf16[1,1,2,1024,1024]{4,3,2,1,0:T(8,128)(2,1)}, u32[]{:S(2)}) copy-start(bf16[1,1,2,1024,1024]{4,3,2,1,0:T(8,128)(2,1)} %param.5) | copy-start | bytes 12582916
  14.5 23.6 %collective-permute-start.3 = (bf16[2,64,512]{2,1,0:T(8,128)(2,1)S(1)}, bf16[2,64,512]{2,1,0:T(8,128)(2,1)S(1)}, u32[]{:S(2)}, u32[]{:S(2)}) collective-permute-start(bf16[2,64,512]{2,1,0:T(8,128)(2,1)S(1)} %collective-permute-done.2), channel_id=1, source_target_pairs={{2,4},{6,8},{10,12},{14,16},{18,20},{22,24},{26,28},{34,36},{38,40... | collective-permute-start | bytes 393224 | tf_op jit(solution)/shard_map/ppermute | solution.py:84
  17.5 2.9 %copy-start.2 = (f32[2,1024]{1,0:T(2,128)S(1)}, f32[2,1024]{1,0:T(2,128)}, u32[]{:S(2)}) copy-start(f32[2,1024]{1,0:T(2,128)} %shard_map.55) | copy-start | bytes 24580
  19.0 19.1 %collective-permute-start.5 = (bf16[2,128,512]{2,1,0:T(8,128)(2,1)S(1)}, bf16[2,128,512]{2,1,0:T(8,128)(2,1)S(1)}, u32[]{:S(2)}, u32[]{:S(2)}) collective-permute-start(bf16[2,128,512]{2,1,0:T(8,128)(2,1)S(1)} %get-tuple-element.41), channel_id=1, source_target_pairs={{1,33},{2,34},{3,35},{5,37},{6,38},{7,39},{9,41},{10,42},{11,43},{... | collective-permute-start | bytes 786440 | tf_op jit(solution)/shard_map/ppermute | solution.py:62
  19.7 18.4 %collective-permute-start.6 = (bf16[2,128,512]{2,1,0:T(8,128)(2,1)S(1)}, bf16[2,128,512]{2,1,0:T(8,128)(2,1)S(1)}, u32[]{:S(2)}, u32[]{:S(2)}) collective-permute-start(bf16[2,128,512]{2,1,0:T(8,128)(2,1)S(1)} %get-tuple-element.42), channel_id=1, source_target_pairs={{1,2},{2,3},{5,6},{6,7},{9,10},{10,11},{13,14},{14,15},{17,18},{18... | collective-permute-start | bytes 786440 | tf_op jit(solution)/shard_map/ppermute | solution.py:66
  41.8 12.8 %collective-permute-start.7 = (bf16[2,128,512]{2,1,0:T(8,128)(2,1)S(1)}, bf16[2,128,512]{2,1,0:T(8,128)(2,1)S(1)}, u32[]{:S(2)}, u32[]{:S(2)}) collective-permute-start(bf16[2,128,512]{2,1,0:T(8,128)(2,1)S(1)} %get-tuple-element.37), channel_id=1, source_target_pairs={{0,32},{4,36},{8,40},{12,44},{16,48},{20,52},{24,56},{28,60},{32,6... | collective-permute-start | bytes 786440 | tf_op jit(solution)/shard_map/ppermute | solution.py:62
  49.0 2.3 %collective-permute-start.9 = (bf16[2,64,512]{2,1,0:T(8,128)(2,1)S(1)}, bf16[2,64,512]{2,1,0:T(8,128)(2,1)S(1)}, u32[]{:S(2)}, u32[]{:S(2)}) collective-permute-start(bf16[2,64,512]{2,1,0:T(8,128)(2,1)S(1)} %get-tuple-element.40), channel_id=1, source_target_pairs={{3,2},{7,6},{11,10},{15,14},{19,18},{23,22},{27,26},{35,34},{39,38... | collective-permute-start | bytes 393224 | tf_op jit(solution)/shard_map/ppermute | solution.py:79
  49.7 29.0 %copy-start.1 = (bf16[1,1,2,1024,1024]{4,3,2,1,0:T(8,128)(2,1)S(1)}, bf16[1,1,2,1024,1024]{4,3,2,1,0:T(8,128)(2,1)}, u32[]{:S(2)}) copy-start(bf16[1,1,2,1024,1024]{4,3,2,1,0:T(8,128)(2,1)} %param.5) | copy-start | bytes 12582916
  49.7 20.1 %collective-permute-start.8 = (bf16[2,64,512]{2,1,0:T(8,128)(2,1)S(1)}, bf16[2,64,512]{2,1,0:T(8,128)(2,1)S(1)}, u32[]{:S(2)}, u32[]{:S(2)}) collective-permute-start(bf16[2,64,512]{2,1,0:T(8,128)(2,1)S(1)} %get-tuple-element.39), channel_id=1, source_target_pairs={{3,4},{7,8},{11,12},{15,16},{19,20},{23,24},{27,28},{35,36},{39,40... | collective-permute-start | bytes 393224 | tf_op jit(solution)/shard_map/ppermute | solution.py:84
  51.2 27.0 %collective-permute-start.10 = (bf16[2,64,512]{2,1,0:T(8,128)(2,1)S(1)}, bf16[2,64,512]{2,1,0:T(8,128)(2,1)S(1)}, u32[]{:S(2)}, u32[]{:S(2)}) collective-permute-start(bf16[2,64,512]{2,1,0:T(8,128)(2,1)S(1)} %collective-permute-done.9), channel_id=1, source_target_pairs={{2,4},{6,8},{10,12},{14,16},{18,20},{22,24},{26,28},{34,36},{38,40... | collective-permute-start | bytes 393224 | tf_op jit(solution)/shard_map/ppermute | solution.py:84
  52.5 25.7 %collective-permute-start.11 = (bf16[2,128,512]{2,1,0:T(8,128)(2,1)S(1)}, bf16[2,128,512]{2,1,0:T(8,128)(2,1)S(1)}, u32[]{:S(2)}, u32[]{:S(2)}) collective-permute-start(bf16[2,128,512]{2,1,0:T(8,128)(2,1)S(1)} %get-tuple-element.38), channel_id=1, source_target_pairs={{0,1},{4,5},{8,9},{12,13},{16,17},{20,21},{24,25},{28,29},{32,33},... | collective-permute-start | bytes 786440 | tf_op jit(solution)/shard_map/ppermute | solution.py:66
  53.9 28.9 %collective-permute-start.14 = (bf16[2,32,512]{2,1,0:T(8,128)(2,1)S(1)}, bf16[2,32,512]{2,1,0:T(8,128)(2,1)S(1)}, u32[]{:S(2)}, u32[]{:S(2)}) collective-permute-start(bf16[2,32,512]{2,1,0:T(8,128)(2,1)S(1)} %get-tuple-element.36), channel_id=1, source_target_pairs={{3,2},{7,6},{11,10},{15,14},{19,18},{23,22},{27,26},{35,34},{39,38... | collective-permute-start | bytes 196616 | tf_op jit(solution)/shard_map/ppermute | solution.py:79
  80.2 21.8 %collective-permute-start.16 = (bf16[2,64,512]{2,1,0:T(8,128)(2,1)S(1)}, bf16[2,64,512]{2,1,0:T(8,128)(2,1)S(1)}, u32[]{:S(2)}, u32[]{:S(2)}) collective-permute-start(bf16[2,64,512]{2,1,0:T(8,128)(2,1)S(1)} %get-tuple-element.34), channel_id=1, source_target_pairs={{0,1},{1,2},{2,3},{4,5},{5,6},{6,7},{8,9},{9,10},{10,11},{12,13},{... | collective-permute-start | bytes 393224 | tf_op jit(solution)/shard_map/ppermute | solution.py:66
  81.5 19.3 %collective-permute-start.13 = (bf16[2,32,512]{2,1,0:T(8,128)(2,1)S(1)}, bf16[2,32,512]{2,1,0:T(8,128)(2,1)S(1)}, u32[]{:S(2)}, u32[]{:S(2)}) collective-permute-start(bf16[2,32,512]{2,1,0:T(8,128)(2,1)S(1)} %get-tuple-element.35), channel_id=1, source_target_pairs={{3,4},{7,8},{11,12},{15,16},{19,20},{23,24},{27,28},{35,36},{39,40... | collective-permute-start | bytes 196616 | tf_op jit(solution)/shard_map/ppermute | solution.py:84
  82.8 19.2 %collective-permute-start.15 = (bf16[2,32,512]{2,1,0:T(8,128)(2,1)S(1)}, bf16[2,32,512]{2,1,0:T(8,128)(2,1)S(1)}, u32[]{:S(2)}, u32[]{:S(2)}) collective-permute-start(bf16[2,32,512]{2,1,0:T(8,128)(2,1)S(1)} %collective-permute-done.14), channel_id=1, source_target_pairs={{2,4},{6,8},{10,12},{14,16},{18,20},{22,24},{26,28},{34,36},{38,40... | collective-permute-start | bytes 196616 | tf_op jit(solution)/shard_map/ppermute | solution.py:84
  84.2 17.9 %collective-permute-start.12 = (bf16[2,64,512]{2,1,0:T(8,128)(2,1)S(1)}, bf16[2,64,512]{2,1,0:T(8,128)(2,1)S(1)}, u32[]{:S(2)}, u32[]{:S(2)}) collective-permute-start(bf16[2,64,512]{2,1,0:T(8,128)(2,1)S(1)} %get-tuple-element.33), channel_id=1, source_target_pairs={{0,32},{1,33},{2,34},{3,35},{4,36},{5,37},{6,38},{7,39},{8,40},{9,... | collective-permute-start | bytes 393224 | tf_op jit(solution)/shard_map/ppermute | solution.py:62

commit v4 on v3

--- a/solution.py
+++ b/solution.py
@@ -10,8 +10,9 @@
 PIECES = {1: ((3, 64), (2, 64)), 2: ((3, 64), (2, 64)), 3: ((3, 32), (2, 32))}
 
 
-def copy_kernel(source_ref, target_ref):
-    target_ref[...] = source_ref[...]
+def split_kernel(factor_ref, real_ref, imag_ref):
+    real_ref[...] = factor_ref[0:1]
+    imag_ref[...] = factor_ref[1:2]
 
 
 def per_device(green_ops, cell_map, dipole_site, dipole_amp, contrast):
@@ -32,6 +33,7 @@
 
     classes = lax.broadcasted_iota(jnp.int32, (contrast.shape[0], 1, rows), 0)
     factor = jnp.where(classes == cells[None], contrast[:, :, None], 0.0).sum(axis=0)
+    factor = (factor[0:1], factor[1:2])
 
     def apply(excited):
         live = excited.shape[1]
@@ -45,7 +47,7 @@
         return jnp.stack([real_out, imag_out]).astype(jnp.bfloat16)
 
     def step(west, south):
-        real_factor, imag_factor = factor[0:1], factor[1:2]
+        real_factor, imag_factor = factor
         incoming = jnp.concatenate([west, south], axis=2).astype(jnp.float32)
         live = incoming.shape[1]
         real_in = real_factor * incoming[0] - imag_factor * incoming[1] + source[0, :live]
@@ -97,9 +99,8 @@
     t2 = step(w2, s2)
     x3 = cross(t2[:, :NB], "x3")
 
-    factor = pl.pallas_call(
-        copy_kernel, out_shape=jax.ShapeDtypeStruct(factor.shape, factor.dtype)
-    )(factor)
+    part = jax.ShapeDtypeStruct((1, rows), jnp.float32)
+    factor = pl.pallas_call(split_kernel, out_shape=(part, part))(jnp.concatenate(factor))
     w1, x1, t2 = lax.optimization_barrier((w1, x1, t2))
     late1 = step(w1, x1)
     w3 = east_to(late1, (0,))

time: 105 us -> 114 us (1.086)
  the two profiles are of different devices: /device:TPU:166 before, /device:TPU:34 now
where the time goes in v4:
time: 114 us; the launch traced here: 113 us
  waiting for transfers between devices  70.6 us (62%)
  starting transfers between devices  23.6 us (21%)
  matrix products  10.2 us (9%)
  other arithmetic  5.39 us (5%)
  local copies, waits for them, and re-layouts  1.65 us (1%)
  Pallas kernels  1.3 us (1%)
    ppermute x6, waiting for transfers between devices, cross(): arrived.append(lax.ppermute(piece, 'gy', pairs))  65.3 us
    dot_general x6, matrix products, apply(): lax.dot_general(flat, operator, (((1,), (2,)), ((), ())), preferred_eleme...  10.2 us
    ppermute x6, starting transfers between devices, cross(): arrived.append(lax.ppermute(piece, 'gy', pairs))  8.02 us
    ppermute x4, starting transfers between devices, east_to(): return lax.ppermute(traces[:, :, :face], ('gx', 'gy'), pairs)  6.84 us
    ppermute x4, starting transfers between devices, north_to(): return lax.ppermute(traces[:, :, face:], 'gy', pairs)  6.78 us
    ppermute x4, waiting for transfers between devices, north_to(): return lax.ppermute(traces[:, :, face:], 'gy', pairs)  3.2 us
  transfers between devices with their start and end apart: 17, of which 8 were waited for; matrix products, arithmetic and copies ran while one was open for 5% of the time, Pallas kernels for 1%

profile of v4, /device:TPU:34, one launch (start us, length us, event | category | flops | bytes accessed | tf_op | source)
XLA Modules:
  0.0 113.4 jit_solution(14290677665644187940)
XLA Ops:
  0.0 0.8 iota_compare_fusion
  0.8 0.0 copy-start.7
  0.8 0.0 copy-start.6
  0.8 0.0 copy-start.8
  0.8 3.5 %fusion.10 = f32[2,128,2,1024]{3,1,2,0:T(8,128)S(1)} fusion(bf16[1,1,2,1024,1024]{4,3,2,1,0:T(8,128)(2,1)} %param.5, f32[2,128]{1,0:T(2,128)} %bitcast.91, pred[128,1024]{1,0:T(8,128)(4,1)S(1)} %iota_compare_fusion), kind=kOutput, calls=%fused_computation.10 | convolution fusion | flops 1074003968 | bytes 6423552 | tf_op jit(solution)/shard_map/dot_general | solution.py:41
  4.3 0.1 fusion.34
  4.5 0.7 collective-permute-start.2
  5.2 3.5 %collective-permute-start.4 = (bf16[2,128,512]{2,1,0:T(8,128)(2,1)S(1)}, bf16[2,128,512]{2,1,0:T(8,128)(2,1)S(1)}, u32[]{:S(2)}, u32[]{:S(2)}) collective-permute-start(bf16[2,128,512]{2,1,0:T(8,128)(2,1)S(1)} %get-tuple-element.47), channel_id=1, source_target_pairs={{0,1},{1,2},{2,3},{4,5},{5,6},{6,7},{8,9},{9,10},{10,11},{12,13},{... | collective-permute-start | bytes 786440 | tf_op jit(solution)/shard_map/ppermute | solution.py:68
  8.7 1.9 %collective-permute-start = (bf16[2,128,512]{2,1,0:T(8,128)(2,1)S(1)}, bf16[2,128,512]{2,1,0:T(8,128)(2,1)S(1)}, u32[]{:S(2)}, u32[]{:S(2)}) collective-permute-start(bf16[2,128,512]{2,1,0:T(8,128)(2,1)S(1)} %get-tuple-element.48), channel_id=1, source_target_pairs={{0,32},{1,33},{2,34},{3,35},{4,36},{5,37},{6,38},{7,39},{8,40},{9,... | collective-permute-start | bytes 786440 | tf_op jit(solution)/shard_map/ppermute | solution.py:64
  10.7 0.1 copy.8
  10.8 0.1 select_reduce_fusion.factor_ref
  10.9 0.0 copy-start.3
  10.9 0.2 broadcast_select_fusion
  11.1 3.2 %collective-permute-done.4 = bf16[2,128,512]{2,1,0:T(8,128)(2,1)S(1)} collective-permute-done((bf16[2,128,512]{2,1,0:T(8,128)(2,1)S(1)}, bf16[2,128,512]{2,1,0:T(8,128)(2,1)S(1)}, u32[]{:S(2)}, u32[]{:S(2)}) %collective-permute-start.4) | collective-permute-done | bytes 262176 | tf_op jit(solution)/shard_map/ppermute | solution.py:68
  14.3 2.2 %collective-permute-done = bf16[2,128,512]{2,1,0:T(8,128)(2,1)S(1)} collective-permute-done((bf16[2,128,512]{2,1,0:T(8,128)(2,1)S(1)}, bf16[2,128,512]{2,1,0:T(8,128)(2,1)S(1)}, u32[]{:S(2)}, u32[]{:S(2)}) %collective-permute-start) | collective-permute-done | bytes 262176 | tf_op jit(solution)/shard_map/ppermute | solution.py:64
  16.4 0.1 maximum_convert_fusion
  16.6 0.2 add_convert_fusion.7
  16.8 1.3 %fusion.8 = f32[2,128,2,1024]{3,1,2,0:T(8,128)S(1)} fusion(bf16[1,1,2,1024,1024]{4,3,2,1,0:T(8,128)(2,1)S(1)} %copy-done, bf16[1,128,1024]{2,1,0:T(8,128)(2,1)S(1)} %get-tuple-element.22, bf16[1,128,1024]{2,1,0:T(8,128)(2,1)S(1)} %get-tuple-element.21), kind=kOutput, calls=%fused_computation.8 | convolution fusion | flops 1074790400 | bytes 6815744 | tf_op jit(solution)/shard_map/dot_general | solution.py:41
  18.1 0.1 fusion.36
  18.3 0.7 collective-permute-start.5
  19.0 0.7 collective-permute-start.6
  19.7 1.3 %collective-permute-start.1 = (bf16[2,64,512]{2,1,0:T(8,128)(2,1)S(1)}, bf16[2,64,512]{2,1,0:T(8,128)(2,1)S(1)}, u32[]{:S(2)}, u32[]{:S(2)}) collective-permute-start(bf16[2,64,512]{2,1,0:T(8,128)(2,1)S(1)} %get-tuple-element.49), channel_id=1, source_target_pairs={{3,4},{7,8},{11,12},{15,16},{19,20},{23,24},{27,28},{35,36},{39,40... | collective-permute-start | bytes 393224 | tf_op jit(solution)/shard_map/ppermute | solution.py:86
  21.0 1.3 %collective-permute-start.3 = (bf16[2,64,512]{2,1,0:T(8,128)(2,1)S(1)}, bf16[2,64,512]{2,1,0:T(8,128)(2,1)S(1)}, u32[]{:S(2)}, u32[]{:S(2)}) collective-permute-start(bf16[2,64,512]{2,1,0:T(8,128)(2,1)S(1)} %collective-permute-done.2), channel_id=1, source_target_pairs={{2,4},{6,8},{10,12},{14,16},{18,20},{22,24},{26,28},{34,36},{38,40... | collective-permute-start | bytes 393224 | tf_op jit(solution)/shard_map/ppermute | solution.py:86
  22.3 1.3 %shard_map.55 = (f32[1,1024]{1,0:T(1,128)}, f32[1,1024]{1,0:T(1,128)}) custom-call(f32[2,1024]{1,0:T(2,128)} %copy-done.3), custom_call_target="tpu_custom_call" | custom-call | tf_op jit(solution)/shard_map/pallas_call | solution.py:103
  23.6 26.9 %collective-permute-done.1 = bf16[2,64,512]{2,1,0:T(8,128)(2,1)S(1)} collective-permute-done((bf16[2,64,512]{2,1,0:T(8,128)(2,1)S(1)}, bf16[2,64,512]{2,1,0:T(8,128)(2,1)S(1)}, u32[]{:S(2)}, u32[]{:S(2)}) %collective-permute-start.1) | collective-permute-done | bytes 131104 | tf_op jit(solution)/shard_map/ppermute | solution.py:86
  50.5 3.1 %collective-permute-done.3 = bf16[2,64,512]{2,1,0:T(8,128)(2,1)S(1)} collective-permute-done((bf16[2,64,512]{2,1,0:T(8,128)(2,1)S(1)}, bf16[2,64,512]{2,1,0:T(8,128)(2,1)S(1)}, u32[]{:S(2)}, u32[]{:S(2)}) %collective-permute-start.3) | collective-permute-done | bytes 131104 | tf_op jit(solution)/shard_map/ppermute | solution.py:86
  53.6 0.1 maximum_convert_fusion.1
  53.7 0.2 add_convert_fusion.5
  54.0 1.3 %fusion.6 = f32[2,128,2,1024]{3,1,2,0:T(8,128)S(1)} fusion(bf16[1,1,2,1024,1024]{4,3,2,1,0:T(8,128)(2,1)S(1)} %copy-done.1, bf16[1,128,1024]{2,1,0:T(8,128)(2,1)S(1)} %get-tuple-element.20, bf16[1,128,1024]{2,1,0:T(8,128)(2,1)S(1)} %get-tuple-element.19), kind=kOutput, calls=%fused_computation.6 | convolution fusion | flops 1074790400 | bytes 6815744 | tf_op jit(solution)/shard_map/dot_general | solution.py:41
  55.3 0.1 fusion.37
  55.4 0.1 pad_maximum_fusion
  55.5 0.1 maximum_convert_fusion.2
  55.6 0.3 copy-done.4
  56.0 0.0 copy-done.5
  56.0 0.2 add_convert_fusion.3
  56.2 1.3 %fusion.4 = f32[2,128,2,1024]{3,1,2,0:T(8,128)S(1)} fusion(bf16[1,1,2,1024,1024]{4,3,2,1,0:T(8,128)(2,1)S(1)} %copy-done.1, bf16[1,128,1024]{2,1,0:T(8,128)(2,1)S(1)} %get-tuple-element.18, bf16[1,128,1024]{2,1,0:T(8,128)(2,1)S(1)} %get-tuple-element.17), kind=kOutput, calls=%fused_computation.4 | convolution fusion | flops 1074790400 | bytes 6815744 | tf_op jit(solution)/shard_map/dot_general | solution.py:41
  57.5 0.1 fusion.39
  57.7 2.3 %collective-permute-start.7 = (bf16[2,128,512]{2,1,0:T(8,128)(2,1)S(1)}, bf16[2,128,512]{2,1,0:T(8,128)(2,1)}, u32[]{:S(2)}, u32[]{:S(2)}) collective-permute-start(bf16[2,128,512]{2,1,0:T(8,128)(2,1)S(1)} %get-tuple-element.41), channel_id=1, source_target_pairs={{0,32},{4,36},{8,40},{12,44},{16,48},{20,52},{24,56},{28,60},{32,6... | collective-permute-start | bytes 786440 | tf_op jit(solution)/shard_map/ppermute | solution.py:64
  60.0 0.7 fusion.54
  60.7 0.7 collective-permute-start.9
  61.4 0.0 copy-start.2
  61.4 1.6 %collective-permute-start.8 = (bf16[2,64,512]{2,1,0:T(8,128)(2,1)S(1)}, bf16[2,64,512]{2,1,0:T(8,128)(2,1)S(1)}, u32[]{:S(2)}, u32[]{:S(2)}) collective-permute-start(bf16[2,64,512]{2,1,0:T(8,128)(2,1)S(1)} %get-tuple-element.43), channel_id=1, source_target_pairs={{3,4},{7,8},{11,12},{15,16},{19,20},{23,24},{27,28},{35,36},{39,40... | collective-permute-start | bytes 393224 | tf_op jit(solution)/shard_map/ppermute | solution.py:86
  63.0 1.3 %collective-permute-start.10 = (bf16[2,64,512]{2,1,0:T(8,128)(2,1)S(1)}, bf16[2,64,512]{2,1,0:T(8,128)(2,1)S(1)}, u32[]{:S(2)}, u32[]{:S(2)}) collective-permute-start(bf16[2,64,512]{2,1,0:T(8,128)(2,1)S(1)} %collective-permute-done.9), channel_id=1, source_target_pairs={{2,4},{6,8},{10,12},{14,16},{18,20},{22,24},{26,28},{34,36},{38,40... | collective-permute-start | bytes 393224 | tf_op jit(solution)/shard_map/ppermute | solution.py:86
  64.3 1.3 %collective-permute-start.11 = (bf16[2,128,512]{2,1,0:T(8,128)(2,1)S(1)}, bf16[2,128,512]{2,1,0:T(8,128)(2,1)S(1)}, u32[]{:S(2)}, u32[]{:S(2)}) collective-permute-start(bf16[2,128,512]{2,1,0:T(8,128)(2,1)S(1)} %get-tuple-element.42), channel_id=1, source_target_pairs={{0,1},{4,5},{8,9},{12,13},{16,17},{20,21},{24,25},{28,29},{32,33},... | collective-permute-start | bytes 786440 | tf_op jit(solution)/shard_map/ppermute | solution.py:68
  65.6 0.7 collective-permute-start.14
  66.3 1.0 broadcast_select_fusion.2
  67.3 18.8 %collective-permute-done.8 = bf16[2,64,512]{2,1,0:T(8,128)(2,1)S(1)} collective-permute-done((bf16[2,64,512]{2,1,0:T(8,128)(2,1)S(1)}, bf16[2,64,512]{2,1,0:T(8,128)(2,1)S(1)}, u32[]{:S(2)}, u32[]{:S(2)}) %collective-permute-start.8) | collective-permute-done | bytes 131104 | tf_op jit(solution)/shard_map/ppermute | solution.py:86
  86.0 1.6 %collective-permute-done.10 = bf16[2,64,512]{2,1,0:T(8,128)(2,1)S(1)} collective-permute-done((bf16[2,64,512]{2,1,0:T(8,128)(2,1)S(1)}, bf16[2,64,512]{2,1,0:T(8,128)(2,1)S(1)}, u32[]{:S(2)}, u32[]{:S(2)}) %collective-permute-start.10) | collective-permute-done | bytes 131104 | tf_op jit(solution)/shard_map/ppermute | solution.py:86
  87.7 0.1 maximum_select_fusion.1
  87.7 0.1 maximum_convert_fusion.3
  87.8 0.2 add_convert_fusion.1
  88.1 1.3 %fusion.2 = f32[2,128,2,1024]{3,1,2,0:T(8,128)S(1)} fusion(bf16[1,1,2,1024,1024]{4,3,2,1,0:T(8,128)(2,1)S(1)} %copy-done.2, bf16[1,128,1024]{2,1,0:T(8,128)(2,1)S(1)} %get-tuple-element.16, bf16[1,128,1024]{2,1,0:T(8,128)(2,1)S(1)} %get-tuple-element.15), kind=kOutput, calls=%fused_computation.2 | convolution fusion | flops 1074790400 | bytes 6815744 | tf_op jit(solution)/shard_map/dot_general | solution.py:41
  89.4 0.1 fusion.41
  89.5 0.1 maximum_select_fusion
  89.6 1.3 %collective-permute-start.16 = (bf16[2,64,512]{2,1,0:T(8,128)(2,1)S(1)}, bf16[2,64,512]{2,1,0:T(8,128)(2,1)S(1)}, u32[]{:S(2)}, u32[]{:S(2)}) collective-permute-start(bf16[2,64,512]{2,1,0:T(8,128)(2,1)S(1)} %get-tuple-element.38), channel_id=1, source_target_pairs={{0,1},{1,2},{2,3},{4,5},{5,6},{6,7},{8,9},{9,10},{10,11},{12,13},{... | collective-permute-start | bytes 393224 | tf_op jit(solution)/shard_map/ppermute | solution.py:68
  90.9 1.3 %collective-permute-start.13 = (bf16[2,32,512]{2,1,0:T(8,128)(2,1)S(1)}, bf16[2,32,512]{2,1,0:T(8,128)(2,1)S(1)}, u32[]{:S(2)}, u32[]{:S(2)}) collective-permute-start(bf16[2,32,512]{2,1,0:T(8,128)(2,1)S(1)} %get-tuple-element.39), channel_id=1, source_target_pairs={{3,4},{7,8},{11,12},{15,16},{19,20},{23,24},{27,28},{35,36},{39,40... | collective-permute-start | bytes 196616 | tf_op jit(solution)/shard_map/ppermute | solution.py:86
  92.3 1.3 %collective-permute-start.15 = (bf16[2,32,512]{2,1,0:T(8,128)(2,1)S(1)}, bf16[2,32,512]{2,1,0:T(8,128)(2,1)S(1)}, u32[]{:S(2)}, u32[]{:S(2)}) collective-permute-start(bf16[2,32,512]{2,1,0:T(8,128)(2,1)S(1)} %collective-permute-done.14), channel_id=1, source_target_pairs={{2,4},{6,8},{10,12},{14,16},{18,20},{22,24},{26,28},{34,36},{38,40... | collective-permute-start | bytes 196616 | tf_op jit(solution)/shard_map/ppermute | solution.py:86
  93.6 1.9 %collective-permute-start.12 = (bf16[2,64,512]{2,1,0:T(8,128)(2,1)S(1)}, bf16[2,64,512]{2,1,0:T(8,128)(2,1)S(1)}, u32[]{:S(2)}, u32[]{:S(2)}) collective-permute-start(bf16[2,64,512]{2,1,0:T(8,128)(2,1)S(1)} %get-tuple-element.37), channel_id=1, source_target_pairs={{0,32},{1,33},{2,34},{3,35},{4,36},{5,37},{6,38},{7,39},{8,40},{9,... | collective-permute-start | bytes 393224 | tf_op jit(solution)/shard_map/ppermute | solution.py:64
  95.5 13.6 %collective-permute-done.13 = bf16[2,32,512]{2,1,0:T(8,128)(2,1)S(1)} collective-permute-done((bf16[2,32,512]{2,1,0:T(8,128)(2,1)S(1)}, bf16[2,32,512]{2,1,0:T(8,128)(2,1)S(1)}, u32[]{:S(2)}, u32[]{:S(2)}) %collective-permute-start.13) | collective-permute-done | bytes 65568 | tf_op jit(solution)/shard_map/ppermute | solution.py:86
  109.1 1.4 %collective-permute-done.15 = bf16[2,32,512]{2,1,0:T(8,128)(2,1)S(1)} collective-permute-done((bf16[2,32,512]{2,1,0:T(8,128)(2,1)S(1)}, bf16[2,32,512]{2,1,0:T(8,128)(2,1)S(1)}, u32[]{:S(2)}, u32[]{:S(2)}) %collective-permute-start.15) | collective-permute-done | bytes 65568 | tf_op jit(solution)/shard_map/ppermute | solution.py:86
  110.5 0.1 fusion.49
  110.6 1.5 %fusion = f32[2,64,2,1024]{3,1,2,0:T(8,128)S(1)} fusion(bf16[1,1,2,1024,1024]{4,3,2,1,0:T(8,128)(2,1)S(1)} %copy-done.2, bf16[1,64,1024]{2,1,0:T(8,128)(2,1)S(1)} %get-tuple-element.34, bf16[1,64,1024]{2,1,0:T(8,128)(2,1)S(1)} %get-tuple-element.33), kind=kOutput, calls=%fused_computation | convolution fusion | flops 537395200 | bytes 5505024 | tf_op jit(solution)/shard_map/dot_general | solution.py:41
  112.2 0.1 fusion.52
  112.3 1.1 copy.9
  (33 shorter events, 0.4 us)
Async XLA Ops:
  0.8 9.9 %copy-start.7 = (f32[3,2]{0,1:T(2,128)S(1)}, f32[3,2]{0,1:T(2,128)}, u32[]{:S(2)}) copy-start(f32[3,2]{0,1:T(2,128)} %param.9) | copy-start | bytes 76
  0.8 10.0 %copy-start.6 = (s32[1,1,1024]{2,1,0:T(1,128)S(1)}, s32[1,1,1024]{2,1,0:T(1,128)}, u32[]{:S(2)}) copy-start(s32[1,1,1024]{2,1,0:T(1,128)} %param.6) | copy-start | bytes 12292
  0.8 10.1 %copy-start.8 = (f32[1,1,2,128]{3,2,1,0:T(2,128)S(1)}, f32[1,1,2,128]{3,2,1,0:T(2,128)}, u32[]{:S(2)}) copy-start(f32[1,1,2,128]{3,2,1,0:T(2,128)} %param.8) | copy-start | bytes 3076
  4.5 16.5 %collective-permute-start.2 = (bf16[2,64,512]{2,1,0:T(8,128)(2,1)S(1)}, bf16[2,64,512]{2,1,0:T(8,128)(2,1)S(1)}, u32[]{:S(2)}, u32[]{:S(2)}) collective-permute-start(bf16[2,64,512]{2,1,0:T(8,128)(2,1)S(1)} %get-tuple-element.50), channel_id=1, source_target_pairs={{3,2},{7,6},{11,10},{15,14},{19,18},{23,22},{27,26},{35,34},{39,38... | collective-permute-start | bytes 393224 | tf_op jit(solution)/shard_map/ppermute | solution.py:81
  5.2 9.0 %collective-permute-start.4 = (bf16[2,128,512]{2,1,0:T(8,128)(2,1)S(1)}, bf16[2,128,512]{2,1,0:T(8,128)(2,1)S(1)}, u32[]{:S(2)}, u32[]{:S(2)}) collective-permute-start(bf16[2,128,512]{2,1,0:T(8,128)(2,1)S(1)} %get-tuple-element.47), channel_id=1, source_target_pairs={{0,1},{1,2},{2,3},{4,5},{5,6},{6,7},{8,9},{9,10},{10,11},{12,13},{... | collective-permute-start | bytes 786440 | tf_op jit(solution)/shard_map/ppermute | solution.py:68
  8.7 7.7 %collective-permute-start = (bf16[2,128,512]{2,1,0:T(8,128)(2,1)S(1)}, bf16[2,128,512]{2,1,0:T(8,128)(2,1)S(1)}, u32[]{:S(2)}, u32[]{:S(2)}) collective-permute-start(bf16[2,128,512]{2,1,0:T(8,128)(2,1)S(1)} %get-tuple-element.48), channel_id=1, source_target_pairs={{0,32},{1,33},{2,34},{3,35},{4,36},{5,37},{6,38},{7,39},{8,40},{9,... | collective-permute-start | bytes 786440 | tf_op jit(solution)/shard_map/ppermute | solution.py:64
  10.8 6.0 %copy-start = (bf16[1,1,2,1024,1024]{4,3,2,1,0:T(8,128)(2,1)S(1)}, bf16[1,1,2,1024,1024]{4,3,2,1,0:T(8,128)(2,1)}, u32[]{:S(2)}) copy-start(bf16[1,1,2,1024,1024]{4,3,2,1,0:T(8,128)(2,1)} %param.5) | copy-start | bytes 12582916
  10.9 7.2 %copy-start.3 = (f32[2,1024]{1,0:T(2,128)}, f32[2,1024]{1,0:T(2,128)S(1)}, u32[]{:S(2)}) copy-start(f32[2,1024]{1,0:T(2,128)S(1)} %select_reduce_fusion.factor_ref) | copy-start | bytes 24580
  18.3 35.3 %collective-permute-start.5 = (bf16[2,128,512]{2,1,0:T(8,128)(2,1)S(1)}, bf16[2,128,512]{2,1,0:T(8,128)(2,1)S(1)}, u32[]{:S(2)}, u32[]{:S(2)}) collective-permute-start(bf16[2,128,512]{2,1,0:T(8,128)(2,1)S(1)} %get-tuple-element.45), channel_id=1, source_target_pairs={{1,33},{2,34},{3,35},{5,37},{6,38},{7,39},{9,41},{10,42},{11,43},{... | collective-permute-start | bytes 786440 | tf_op jit(solution)/shard_map/ppermute | solution.py:64
  19.0 34.6 %collective-permute-start.6 = (bf16[2,128,512]{2,1,0:T(8,128)(2,1)S(1)}, bf16[2,128,512]{2,1,0:T(8,128)(2,1)S(1)}, u32[]{:S(2)}, u32[]{:S(2)}) collective-permute-start(bf16[2,128,512]{2,1,0:T(8,128)(2,1)S(1)} %get-tuple-element.46), channel_id=1, source_target_pairs={{1,2},{2,3},{5,6},{6,7},{9,10},{10,11},{13,14},{14,15},{17,18},{18... | collective-permute-start | bytes 786440 | tf_op jit(solution)/shard_map/ppermute | solution.py:68
  19.7 30.8 %collective-permute-start.1 = (bf16[2,64,512]{2,1,0:T(8,128)(2,1)S(1)}, bf16[2,64,512]{2,1,0:T(8,128)(2,1)S(1)}, u32[]{:S(2)}, u32[]{:S(2)}) collective-permute-start(bf16[2,64,512]{2,1,0:T(8,128)(2,1)S(1)} %get-tuple-element.49), channel_id=1, source_target_pairs={{3,4},{7,8},{11,12},{15,16},{19,20},{23,24},{27,28},{35,36},{39,40... | collective-permute-start | bytes 393224 | tf_op jit(solution)/shard_map/ppermute | solution.py:86
  21.0 32.6 %collective-permute-start.3 = (bf16[2,64,512]{2,1,0:T(8,128)(2,1)S(1)}, bf16[2,64,512]{2,1,0:T(8,128)(2,1)S(1)}, u32[]{:S(2)}, u32[]{:S(2)}) collective-permute-start(bf16[2,64,512]{2,1,0:T(8,128)(2,1)S(1)} %collective-permute-done.2), channel_id=1, source_target_pairs={{2,4},{6,8},{10,12},{14,16},{18,20},{22,24},{26,28},{34,36},{38,40... | collective-permute-start | bytes 393224 | tf_op jit(solution)/shard_map/ppermute | solution.py:86
  23.6 30.4 %copy-start.1 = (bf16[1,1,2,1024,1024]{4,3,2,1,0:T(8,128)(2,1)S(1)}, bf16[1,1,2,1024,1024]{4,3,2,1,0:T(8,128)(2,1)}, u32[]{:S(2)}) copy-start(bf16[1,1,2,1024,1024]{4,3,2,1,0:T(8,128)(2,1)} %param.5) | copy-start | bytes 12582916
  55.3 0.7 copy-start.4
  55.3 0.7 copy-start.5
  57.7 8.6 %collective-permute-start.7 = (bf16[2,128,512]{2,1,0:T(8,128)(2,1)S(1)}, bf16[2,128,512]{2,1,0:T(8,128)(2,1)}, u32[]{:S(2)}, u32[]{:S(2)}) collective-permute-start(bf16[2,128,512]{2,1,0:T(8,128)(2,1)S(1)} %get-tuple-element.41), channel_id=1, source_target_pairs={{0,32},{4,36},{8,40},{12,44},{16,48},{20,52},{24,56},{28,60},{32,6... | collective-permute-start | bytes 786440 | tf_op jit(solution)/shard_map/ppermute | solution.py:64
  60.7 2.3 %collective-permute-start.9 = (bf16[2,64,512]{2,1,0:T(8,128)(2,1)}, bf16[2,64,512]{2,1,0:T(8,128)(2,1)S(1)}, u32[]{:S(2)}, u32[]{:S(2)}) collective-permute-start(bf16[2,64,512]{2,1,0:T(8,128)(2,1)} %get-tuple-element.44), channel_id=1, source_target_pairs={{3,2},{7,6},{11,10},{15,14},{19,18},{23,22},{27,26},{35,34},{39,38... | collective-permute-start | bytes 393224 | tf_op jit(solution)/shard_map/ppermute | solution.py:81
  61.4 26.7 %copy-start.2 = (bf16[1,1,2,1024,1024]{4,3,2,1,0:T(8,128)(2,1)S(1)}, bf16[1,1,2,1024,1024]{4,3,2,1,0:T(8,128)(2,1)}, u32[]{:S(2)}) copy-start(bf16[1,1,2,1024,1024]{4,3,2,1,0:T(8,128)(2,1)} %param.5) | copy-start | bytes 12582916
  61.4 24.6 %collective-permute-start.8 = (bf16[2,64,512]{2,1,0:T(8,128)(2,1)S(1)}, bf16[2,64,512]{2,1,0:T(8,128)(2,1)S(1)}, u32[]{:S(2)}, u32[]{:S(2)}) collective-permute-start(bf16[2,64,512]{2,1,0:T(8,128)(2,1)S(1)} %get-tuple-element.43), channel_id=1, source_target_pairs={{3,4},{7,8},{11,12},{15,16},{19,20},{23,24},{27,28},{35,36},{39,40... | collective-permute-start | bytes 393224 | tf_op jit(solution)/shard_map/ppermute | solution.py:86
  63.0 24.7 %collective-permute-start.10 = (bf16[2,64,512]{2,1,0:T(8,128)(2,1)S(1)}, bf16[2,64,512]{2,1,0:T(8,128)(2,1)S(1)}, u32[]{:S(2)}, u32[]{:S(2)}) collective-permute-start(bf16[2,64,512]{2,1,0:T(8,128)(2,1)S(1)} %collective-permute-done.9), channel_id=1, source_target_pairs={{2,4},{6,8},{10,12},{14,16},{18,20},{22,24},{26,28},{34,36},{38,40... | collective-permute-start | bytes 393224 | tf_op jit(solution)/shard_map/ppermute | solution.py:86
  64.3 23.4 %collective-permute-start.11 = (bf16[2,128,512]{2,1,0:T(8,128)(2,1)S(1)}, bf16[2,128,512]{2,1,0:T(8,128)(2,1)S(1)}, u32[]{:S(2)}, u32[]{:S(2)}) collective-permute-start(bf16[2,128,512]{2,1,0:T(8,128)(2,1)S(1)} %get-tuple-element.42), channel_id=1, source_target_pairs={{0,1},{4,5},{8,9},{12,13},{16,17},{20,21},{24,25},{28,29},{32,33},... | collective-permute-start | bytes 786440 | tf_op jit(solution)/shard_map/ppermute | solution.py:68
  65.6 26.6 %collective-permute-start.14 = (bf16[2,32,512]{2,1,0:T(8,128)(2,1)S(1)}, bf16[2,32,512]{2,1,0:T(8,128)(2,1)S(1)}, u32[]{:S(2)}, u32[]{:S(2)}) collective-permute-start(bf16[2,32,512]{2,1,0:T(8,128)(2,1)S(1)} %get-tuple-element.40), channel_id=1, source_target_pairs={{3,2},{7,6},{11,10},{15,14},{19,18},{23,22},{27,26},{35,34},{39,38... | collective-permute-start | bytes 196616 | tf_op jit(solution)/shard_map/ppermute | solution.py:81
  89.6 20.8 %collective-permute-start.16 = (bf16[2,64,512]{2,1,0:T(8,128)(2,1)S(1)}, bf16[2,64,512]{2,1,0:T(8,128)(2,1)S(1)}, u32[]{:S(2)}, u32[]{:S(2)}) collective-permute-start(bf16[2,64,512]{2,1,0:T(8,128)(2,1)S(1)} %get-tuple-element.38), channel_id=1, source_target_pairs={{0,1},{1,2},{2,3},{4,5},{5,6},{6,7},{8,9},{9,10},{10,11},{12,13},{... | collective-permute-start | bytes 393224 | tf_op jit(solution)/shard_map/ppermute | solution.py:68
  90.9 18.1 %collective-permute-start.13 = (bf16[2,32,512]{2,1,0:T(8,128)(2,1)S(1)}, bf16[2,32,512]{2,1,0:T(8,128)(2,1)S(1)}, u32[]{:S(2)}, u32[]{:S(2)}) collective-permute-start(bf16[2,32,512]{2,1,0:T(8,128)(2,1)S(1)} %get-tuple-element.39), channel_id=1, source_target_pairs={{3,4},{7,8},{11,12},{15,16},{19,20},{23,24},{27,28},{35,36},{39,40... | collective-permute-start | bytes 196616 | tf_op jit(solution)/shard_map/ppermute | solution.py:86
  92.3 18.2 %collective-permute-start.15 = (bf16[2,32,512]{2,1,0:T(8,128)(2,1)S(1)}, bf16[2,32,512]{2,1,0:T(8,128)(2,1)S(1)}, u32[]{:S(2)}, u32[]{:S(2)}) collective-permute-start(bf16[2,32,512]{2,1,0:T(8,128)(2,1)S(1)} %collective-permute-done.14), channel_id=1, source_target_pairs={{2,4},{6,8},{10,12},{14,16},{18,20},{22,24},{26,28},{34,36},{38,40... | collective-permute-start | bytes 196616 | tf_op jit(solution)/shard_map/ppermute | solution.py:86
  93.6 16.9 %collective-permute-start.12 = (bf16[2,64,512]{2,1,0:T(8,128)(2,1)S(1)}, bf16[2,64,512]{2,1,0:T(8,128)(2,1)S(1)}, u32[]{:S(2)}, u32[]{:S(2)}) collective-permute-start(bf16[2,64,512]{2,1,0:T(8,128)(2,1)S(1)} %get-tuple-element.37), channel_id=1, source_target_pairs={{0,32},{1,33},{2,34},{3,35},{4,36},{5,37},{6,38},{7,39},{8,40},{9,... | collective-permute-start | bytes 393224 | tf_op jit(solution)/shard_map/ppermute | solution.py:64
